TPU v7x, 256 devices: a whole 4x4x8 slice. The times are simulated.
256 devices in a mesh: tm: 8 (over x, core), gx: 4 (over y), gy: 8 (over z).
Axes of the slice: x: 4, y: 4, z: 8, core: 2. Of those that a mesh axis runs over, the one named last changes fastest.
Arguments:
- trajectory: float32 [16, 3, 256, 1024], P('tm', None, 'gy', 'gx'), may hold values from -3 to 3
- initial: float32 [3, 256, 1024], P(None, 'gy', 'gx'), may hold values from -3 to 3
Outputs:
- updated: float32 [16, 3, 256, 1024], P('tm', None, 'gy', 'gx')
- residual: float32 [16, 3, 256, 1024], P('tm', None, 'gy', 'gx')
All inputs are finite; a program needn't handle non-finite values.
Results may differ from a plain program's by a relative error of at most 0.00023.
Values sent between devices are 32-bit elements; how exact they have to be, the bound alone decides.
A program may use at most 64 MiB of HBM per device.

v0:
```python
import math

import jax
import jax.numpy as jnp
from jax import lax
from jax.sharding import PartitionSpec as P

CHEB = 6


courant_x = 1.5
courant_y = 1.5
coriolis_mean = 0.3
coriolis_slope = 0.4
circulant = 0.1
spectrum_edge = 5.0
highest = lax.Precision.HIGHEST


def passed_along(value, axis, steps):
    count = lax.axis_size(axis)
    first, last = (max(0, -steps), min(count, count - steps))
    return lax.ppermute(value, axis, [(source, source + steps) for source in range(first, last)])


def with_halo(array, sides, width):
    edges = {}
    for axis, dim in sides:
        count, length = (lax.axis_size(axis), array.shape[dim])
        up = [(i, (i + 1) % count) for i in range(count)]
        last = lax.slice_in_dim(array, length - width, length, axis=dim)
        first = lax.slice_in_dim(array, 0, width, axis=dim)
        edges[dim] = (
            lax.ppermute(last, axis, up),
            lax.ppermute(first, axis, [(b, a) for a, b in up]),
        )
    done = []
    for _, dim in sides:
        low, high = edges[dim]
        around = [(width, width) if d in done else (0, 0) for d in range(array.ndim)]
        array = jnp.concatenate([jnp.pad(low, around), array, jnp.pad(high, around)], axis=dim)
        done.append(dim)
    return array


def in_blocks(array, dim, count):
    before, after = (array.shape[:dim], array.shape[dim + 1 :])
    return jnp.moveaxis(array.reshape(*before, count, -1, *after), dim, 0)


def sent_and_summed(array, axis, dim):
    count = lax.axis_size(axis)
    pieces = lax.all_to_all(in_blocks(array, dim, count), axis, 0, 0, tiled=True)
    return jnp.sum(pieces, axis=0)


def with_halo_2(array, sides, width):
    for axis, dim in sides:
        count, length = (lax.axis_size(axis), array.shape[dim])
        up = [(i, (i + 1) % count) for i in range(count)]
        down = [(j, i) for i, j in up]
        last = lax.slice_in_dim(array, length - width, length, axis=dim)
        first = lax.slice_in_dim(array, 0, width, axis=dim)
        before = lax.ppermute(last, axis, up)
        after = lax.ppermute(first, axis, down)
        array = jnp.concatenate([before, array, after], axis=dim)
    return array


def along_lon(padded):
    return padded[..., 1:-1, 2:] - padded[..., 1:-1, :-2]


def along_lat(padded):
    return padded[..., 2:, 1:-1] - padded[..., :-2, 1:-1]


def inner(padded):
    return padded[..., 1:-1, 1:-1]


def crop_cycle(values, margin):
    return values[..., margin : values.shape[-2] - margin, margin : values.shape[-1] - margin]


def coriolis(start, count, extent):
    latitude = ((start + lax.iota(jnp.int32, count)) % extent).astype(jnp.float32)
    return (coriolis_mean + coriolis_slope * ((latitude + 0.5) / extent - 0.5))[:, None]


def wave(padded, rotation):
    height, eastward, northward = (padded[..., 0, :, :], padded[..., 1, :, :], padded[..., 2, :, :])
    height_rate = courant_x * along_lon(eastward) + courant_y * along_lat(northward)
    east_rate = courant_x * along_lon(height) - rotation * inner(northward)
    north_rate = courant_y * along_lat(height) + rotation * inner(eastward)
    return jnp.stack([height_rate, east_rate, north_rate], axis=-3)


def advect(padded):
    height, eastward, northward = (padded[..., 0, :, :], padded[..., 1, :, :], padded[..., 2, :, :])
    east_mid = inner(eastward)
    north_mid = inner(northward)
    height_rate = courant_x * along_lon(height * eastward) + courant_y * along_lat(
        height * northward
    )
    east_rate = east_mid * (courant_x * along_lon(eastward)) + north_mid * (
        courant_y * along_lat(eastward)
    )
    north_rate = east_mid * (courant_x * along_lon(northward)) + north_mid * (
        courant_y * along_lat(northward)
    )
    return jnp.stack([height_rate, east_rate, north_rate], axis=-3)


def phase_table(rows, columns, total):
    products = rows[:, None] * columns[None, :] % total
    return 2.0 * math.pi / total * products.astype(jnp.float32)


def time_weights(times, total, signed):
    return jnp.exp(signed * math.log(circulant) / total * times.astype(jnp.float32))


def frequency_shift(frequency, total):
    factor = math.exp(math.log(circulant) / total)
    angle = 2.0 * math.pi / total * frequency.astype(jnp.float32)
    return (1.0 - factor * jnp.cos(angle), factor * jnp.sin(angle))


def complex_times(first, second):
    return (
        first[0] * second[0] - first[1] * second[1],
        first[0] * second[1] + first[1] * second[0],
    )


def complex_divide(first, second):
    denominator = second[0] * second[0] + second[1] * second[1]
    return (
        (first[0] * second[0] + first[1] * second[1]) / denominator,
        (first[1] * second[0] - first[0] * second[1]) / denominator,
    )


def cheb_turn(rhs, shift, solution, update, turned, sigma, rho_old):
    shifted = complex_times(shift, solution)
    misfit = (rhs[0] - (shifted[0] + turned[0]), rhs[1] - (shifted[1] + turned[1]))
    rho_new = complex_divide((1.0, 0.0), (2.0 * sigma[0] - rho_old[0], 2.0 * sigma[1] - rho_old[1]))
    carry_coef = complex_times(rho_new, rho_old)
    misfit_coef = complex_divide((2.0 * rho_new[0], 2.0 * rho_new[1]), (0.0, spectrum_edge))
    first_part = complex_times(carry_coef, update)
    second_part = complex_times(misfit_coef, misfit)
    update = (first_part[0] + second_part[0], first_part[1] + second_part[1])
    solution = (solution[0] + update[0], solution[1] + update[1])
    return (solution, update, rho_new)


def shards(trajectory, initial):
    local_steps, fieldcount, rows_lat, rows_lon = trajectory.shape
    total = local_steps * lax.axis_size("tm")
    times = lax.axis_index("tm") * local_steps + lax.iota(jnp.int32, local_steps)
    nlat = rows_lat * lax.axis_size("gy")
    lat_start = lax.axis_index("gy") * rows_lat
    rotation = coriolis(lat_start, rows_lat, nlat)
    carried = passed_along(trajectory[-1], "tm", 1)
    opening = jnp.where(lax.axis_index("tm") == 0, initial, carried)
    previous = jnp.concatenate([opening[None], trajectory[:-1]], axis=0)
    padded = with_halo(trajectory, (("gx", 3), ("gy", 2)), 1)
    residual = trajectory - previous + wave(padded, rotation) + advect(padded)
    scaled = residual * time_weights(times, total, 1.0)[:, None, None, None]
    whole_local = scaled.reshape(local_steps, -1)
    count = local_steps * lax.axis_size("tm")
    frequency = lax.iota(jnp.int32, count)
    table = phase_table(frequency, times, total)
    real = jnp.dot(jnp.cos(table), whole_local, precision=highest).reshape(
        count, fieldcount, rows_lat, rows_lon
    )
    imag = (-jnp.dot(jnp.sin(table), whole_local, precision=highest)).reshape(
        count, fieldcount, rows_lat, rows_lon
    )
    stacked = sent_and_summed(jnp.concatenate([real, imag], axis=1), "tm", 0)
    spec_re = stacked[:, :fieldcount]
    spec_im = stacked[:, fieldcount:]
    shift = frequency_shift(times[:, None, None, None], total)
    deep = with_halo_2(jnp.stack([spec_re, spec_im]), (("gx", 4), ("gy", 3)), CHEB)
    rotation_wide = coriolis(lat_start - CHEB, rows_lat + 2 * CHEB, nlat)
    rhs = (deep[0], deep[1])
    sigma = complex_divide(shift, (0.0, spectrum_edge))
    rho_old = complex_divide((1.0, 0.0), sigma)
    update = complex_divide(rhs, shift)
    solution = update
    for iteration in range(CHEB):
        margin = iteration + 1
        rotation_now = rotation_wide[margin : rotation_wide.shape[0] - margin]
        rates = wave(jnp.stack([solution[0], solution[1]]), rotation_now)
        turned = (rates[0], rates[1])
        rhs = (crop_cycle(rhs[0], 1), crop_cycle(rhs[1], 1))
        solution = (crop_cycle(solution[0], 1), crop_cycle(solution[1], 1))
        update = (crop_cycle(update[0], 1), crop_cycle(update[1], 1))
        solution, update, rho_old = cheb_turn(rhs, shift, solution, update, turned, sigma, rho_old)
    sol_re, sol_im = solution
    real_local = sol_re.reshape(local_steps, -1)
    imag_local = sol_im.reshape(local_steps, -1)
    count = local_steps * lax.axis_size("tm")
    rows = lax.iota(jnp.int32, count)
    table = phase_table(rows, times, total)
    values = jnp.dot(jnp.cos(table), real_local, precision=highest) - jnp.dot(
        jnp.sin(table), imag_local, precision=highest
    )
    back = sent_and_summed(values.reshape(count, fieldcount, rows_lat, rows_lon), "tm", 0) / total
    correction = back * time_weights(times, total, -1.0)[:, None, None, None]
    return (trajectory - correction, residual)


def solution(mesh):
    in_specs = (P("tm", None, "gy", "gx"), P(None, "gy", "gx"))
    out_specs = (P("tm", None, "gy", "gx"), P("tm", None, "gy", "gx"))
    return jax.shard_map(shards, mesh=mesh, in_specs=in_specs, out_specs=out_specs, check_vma=False)
```

profile of v0, /device:TPU:1, one launch (start us, length us, event | category | flops | bytes accessed | tf_op | source)
XLA Modules:
  0.0 130.7 jit_solution(12647595976735855362)
XLA Ops:
  0.6 1.0 fusion.195
  1.7 2.2 %collective-permute-start.2 = (f32[2,3,32,1]{3,2,0,1:T(8,128)S(1)}, f32[2,3,32,1]{3,2,0,1:T(8,128)S(1)}, u32[]{:S(2)}, u32[]{:S(2)}) collective-permute-start(f32[2,3,32,1]{3,2,0,1:T(8,128)S(1)} %get-tuple-element.91), channel_id=1, source_target_pairs={{0,8},{8,16},{16,24},{24,0},{1,9},{9,17},{17,25},{25,1},{2,10},{10... | collective-permute-start | bytes 2312 | tf_op jit(solution)/shard_map/ppermute | solution.py:34
  3.9 1.5 %collective-permute-start.3 = (f32[2,3,32,1]{3,2,0,1:T(8,128)S(1)}, f32[2,3,32,1]{3,2,0,1:T(8,128)S(1)}, u32[]{:S(2)}, u32[]{:S(2)}) collective-permute-start(f32[2,3,32,1]{3,2,0,1:T(8,128)S(1)} %get-tuple-element.92), channel_id=1, source_target_pairs={{8,0},{16,8},{24,16},{0,24},{9,1},{17,9},{25,17},{1,25},{10,2},{18... | collective-permute-start | bytes 2312 | tf_op jit(solution)/shard_map/ppermute | solution.py:35
  5.4 0.8 fusion.196
  6.2 1.7 %collective-permute-start.1 = (f32[2,3,1,256]{3,2,0,1:T(1,128)S(1)}, f32[2,3,1,256]{3,2,0,1:T(1,128)S(1)}, u32[]{:S(2)}, u32[]{:S(2)}) collective-permute-start(f32[2,3,1,256]{3,2,0,1:T(1,128)S(1)} %get-tuple-element.93), channel_id=1, source_target_pairs={{0,1},{1,2},{2,3},{3,4},{4,5},{5,6},{6,7},{7,0},{8,9},{9,10},{10,1... | collective-permute-start | bytes 18440 | tf_op jit(solution)/shard_map/ppermute | solution.py:34
  7.9 4.0 %collective-permute-start.4 = (f32[2,3,1,256]{3,2,0,1:T(1,128)S(1)}, f32[2,3,1,256]{3,2,0,1:T(1,128)S(1)}, u32[]{:S(2)}, u32[]{:S(2)}) collective-permute-start(f32[2,3,1,256]{3,2,0,1:T(1,128)S(1)} %get-tuple-element.94), channel_id=1, source_target_pairs={{1,0},{2,1},{3,2},{4,3},{5,4},{6,5},{7,6},{0,7},{9,8},{10,9},{11,1... | collective-permute-start | bytes 18440 | tf_op jit(solution)/shard_map/ppermute | solution.py:35
  12.0 0.9 slice_bitcast_fusion.17
  12.9 4.4 %collective-permute-start = (f32[3,32,256]{2,1,0:T(8,128)S(1)}, f32[3,32,256]{2,1,0:T(8,128)S(1)}, u32[]{:S(2)}, u32[]{:S(2)}) collective-permute-start(f32[3,32,256]{2,1,0:T(8,128)S(1)} %slice_bitcast_fusion.17), channel_id=1, source_target_pairs={{0,32},{32,64},{64,96},{96,128},{128,160},{160,192},{192,224},{1,3... | collective-permute-start | bytes 294920 | tf_op jit(solution)/shard_map/ppermute | solution.py:23
  17.3 0.9 slice.687
  18.2 1.2 select_maximum_fusion
  20.4 0.7 broadcast_multiply_fusion
  21.3 1.4 %convolution_negate_fusion = f32[16,24576]{1,0:T(8,128)S(1)} fusion(f32[2,24576]{1,0:T(2,128)S(1)} %bitcast.304, s32[2]{0:T(128)S(1)} %iota_add_fusion), kind=kOutput, calls=%fused_computation.1 | convolution fusion | flops 9830848 | bytes 1769480 | tf_op jit(solution)/shard_map/dot_general | solution.py:178
  23.2 0.9 copy.89
  24.1 1.5 %fusion.147 = f32[8,2,3,32,256]{4,0,3,2,1:T(8,128)S(1)} fusion(f32[3,32,256,2,1]{2,3,1,0,4:T(2,128)S(1)} %bitcast.305, s32[8,2]{0,1:T(2,128)S(1)} %multiply_add_fusion, s32[2]{0:T(128)S(1)} %iota_add_fusion), kind=kOutput, calls=%fused_computation.307 | convolution fusion | flops 9437632 | bytes 1769544 | tf_op jit(solution)/shard_map/dot_general | solution.py:175
  25.9 2.6 %copy.90 = f32[8,2,6,32,256]{4,3,2,1,0:T(8,128)} copy(f32[8,2,6,32,256]{4,0,3,2,1:T(8,128)S(1)} %pad_maximum_fusion) | data formatting | bytes 6291456 | tf_op jit(solution)/shard_map/concatenate | solution.py:181
  28.4 4.1 %all-to-all-start = ((f32[8,2,6,32,256]{4,3,2,1,0:T(8,128)}), f32[8,2,6,32,256]{4,3,2,1,0:T(8,128)S(1)}, u32[]{:S(2)}, u32[]{:S(2)}) async-start(f32[8,2,6,32,256]{4,3,2,1,0:T(8,128)} %copy.90), calls=%async_computation | async-start | bytes 6291456 | tf_op jit(solution)/shard_map/all_to_all | solution.py:53
  33.8 36.2 %all-to-all-done = f32[8,2,6,32,256]{4,3,2,1,0:T(8,128)S(1)} async-done(((f32[8,2,6,32,256]{4,3,2,1,0:T(8,128)}), f32[8,2,6,32,256]{4,3,2,1,0:T(8,128)S(1)}, u32[]{:S(2)}, u32[]{:S(2)}) %all-to-all-start) | async-done | bytes 3145760 | tf_op jit(solution)/shard_map/all_to_all | solution.py:53
  70.0 1.0 reduce_sum.18
  71.0 1.0 slice_bitcast_fusion.13
  72.4 2.6 %collective-permute-start.6 = (f32[2,2,3,32,6]{4,3,2,1,0:T(8,128)S(1)}, f32[2,2,3,32,6]{4,3,2,1,0:T(8,128)S(1)}, u32[]{:S(2)}, u32[]{:S(2)}) collective-permute-start(f32[2,2,3,32,6]{4,3,2,1,0:T(8,128)S(1)} %get-tuple-element.62), channel_id=1, source_target_pairs={{8,0},{16,8},{24,16},{0,24},{9,1},{17,9},{25,17},{1,25},{10,2},{18... | collective-permute-start | bytes 27656 | tf_op jit(solution)/shard_map/ppermute | solution.py:65
  75.4 3.6 %collective-permute-done.5 = f32[2,2,3,32,6]{4,3,2,1,0:T(8,128)S(1)} collective-permute-done((f32[2,2,3,32,6]{4,3,2,1,0:T(8,128)S(1)}, f32[2,2,3,32,6]{4,3,2,1,0:T(8,128)S(1)}, u32[]{:S(2)}, u32[]{:S(2)}) %collective-permute-start.5) | collective-permute-done | bytes 9248 | tf_op jit(solution)/shard_map/ppermute | solution.py:64
  79.3 2.7 %collective-permute-start.8 = (f32[2,2,3,6,268]{4,3,2,1,0:T(8,128)S(1)}, f32[2,2,3,6,268]{4,3,2,1,0:T(8,128)S(1)}, u32[]{:S(2)}, u32[]{:S(2)}) collective-permute-start(f32[2,2,3,6,268]{4,3,2,1,0:T(8,128)S(1)} %get-tuple-element.46), channel_id=1, source_target_pairs={{1,0},{2,1},{3,2},{4,3},{5,4},{6,5},{7,6},{0,7},{9,8},{10,9},{11,1... | collective-permute-start | bytes 231560 | tf_op jit(solution)/shard_map/ppermute | solution.py:65
  82.0 2.5 %collective-permute-done.7 = f32[2,2,3,6,268]{4,3,2,1,0:T(8,128)S(1)} collective-permute-done((f32[2,2,3,6,268]{4,3,2,1,0:T(8,128)S(1)}, f32[2,2,3,6,268]{4,3,2,1,0:T(8,128)S(1)}, u32[]{:S(2)}, u32[]{:S(2)}) %collective-permute-start.7) | collective-permute-done | bytes 77216 | tf_op jit(solution)/shard_map/ppermute | solution.py:64
  87.9 0.7 fusion.35
  89.4 0.6 fusion.92
  92.9 0.6 fusion.72
  98.0 1.4 %fusion.133 = f32[16,24576]{1,0:T(8,128)S(1)} fusion(f32[2,24576]{1,0:T(2,128)S(1)} %bitcast.310, s32[2]{0:T(128)S(1)} %iota_add_fusion), kind=kOutput, calls=%fused_computation.288 | convolution fusion | flops 9437632 | bytes 1769480 | tf_op jit(solution)/shard_map/dot_general | solution.py:207
  99.6 1.4 %convolution_subtract_fusion = f32[16,24576]{1,0:T(8,128)S(1)} fusion(f32[16,24576]{1,0:T(8,128)S(1)} %fusion.133, f32[2,24576]{1,0:T(2,128)S(1)} %bitcast.306, s32[2]{0:T(128)S(1)} %iota_add_fusion), kind=kOutput, calls=%fused_computation | convolution fusion | flops 9830848 | bytes 3342344 | tf_op jit(solution)/shard_map/dot_general | solution.py:207
  101.0 1.7 %copy.165 = f32[2,8,96,256]{3,2,1,0:T(8,128)} copy(f32[2,8,96,256]{3,1,2,0:T(8,128)S(1)} %bitcast.291) | data formatting | bytes 3145728
  102.7 6.5 %all-to-all-start.1 = ((f32[8,2,3,32,256]{4,3,2,1,0:T(8,128)}), f32[8,2,3,32,256]{4,3,2,1,0:T(8,128)S(1)}, u32[]{:S(2)}, u32[]{:S(2)}) async-start(f32[8,2,3,32,256]{4,3,2,1,0:T(8,128)} %bitcast.135), calls=%async_computation.1 | async-start | bytes 3145728 | tf_op jit(solution)/shard_map/all_to_all | solution.py:53
  109.2 20.6 %all-to-all-done.1 = f32[8,2,3,32,256]{4,3,2,1,0:T(8,128)S(1)} async-done(((f32[8,2,3,32,256]{4,3,2,1,0:T(8,128)}), f32[8,2,3,32,256]{4,3,2,1,0:T(8,128)S(1)}, u32[]{:S(2)}, u32[]{:S(2)}) %all-to-all-start.1) | async-done | bytes 1572896 | tf_op jit(solution)/shard_map/all_to_all | solution.py:53
  129.9 0.8 multiply_subtract_fusion
  (93 shorter events, 15.7 us)
Async XLA Ops:
  1.7 16.5 %collective-permute-start.2 = (f32[2,3,32,1]{3,2,0,1:T(8,128)S(1)}, f32[2,3,32,1]{3,2,0,1:T(8,128)S(1)}, u32[]{:S(2)}, u32[]{:S(2)}) collective-permute-start(f32[2,3,32,1]{3,2,0,1:T(8,128)S(1)} %get-tuple-element.91), channel_id=1, source_target_pairs={{0,8},{8,16},{16,24},{24,0},{1,9},{9,17},{17,25},{25,1},{2,10},{10... | collective-permute-start | bytes 2312 | tf_op jit(solution)/shard_map/ppermute | solution.py:34
  3.9 14.4 %collective-permute-start.3 = (f32[2,3,32,1]{3,2,0,1:T(8,128)S(1)}, f32[2,3,32,1]{3,2,0,1:T(8,128)S(1)}, u32[]{:S(2)}, u32[]{:S(2)}) collective-permute-start(f32[2,3,32,1]{3,2,0,1:T(8,128)S(1)} %get-tuple-element.92), channel_id=1, source_target_pairs={{8,0},{16,8},{24,16},{0,24},{9,1},{17,9},{25,17},{1,25},{10,2},{18... | collective-permute-start | bytes 2312 | tf_op jit(solution)/shard_map/ppermute | solution.py:35
  6.2 12.0 %collective-permute-start.1 = (f32[2,3,1,256]{3,2,0,1:T(1,128)S(1)}, f32[2,3,1,256]{3,2,0,1:T(1,128)S(1)}, u32[]{:S(2)}, u32[]{:S(2)}) collective-permute-start(f32[2,3,1,256]{3,2,0,1:T(1,128)S(1)} %get-tuple-element.93), channel_id=1, source_target_pairs={{0,1},{1,2},{2,3},{3,4},{4,5},{5,6},{6,7},{7,0},{8,9},{9,10},{10,1... | collective-permute-start | bytes 18440 | tf_op jit(solution)/shard_map/ppermute | solution.py:34
  7.9 10.3 %collective-permute-start.4 = (f32[2,3,1,256]{3,2,0,1:T(1,128)S(1)}, f32[2,3,1,256]{3,2,0,1:T(1,128)S(1)}, u32[]{:S(2)}, u32[]{:S(2)}) collective-permute-start(f32[2,3,1,256]{3,2,0,1:T(1,128)S(1)} %get-tuple-element.94), channel_id=1, source_target_pairs={{1,0},{2,1},{3,2},{4,3},{5,4},{6,5},{7,6},{0,7},{9,8},{10,9},{11,1... | collective-permute-start | bytes 18440 | tf_op jit(solution)/shard_map/ppermute | solution.py:35
  12.9 7.2 %collective-permute-start = (f32[3,32,256]{2,1,0:T(8,128)S(1)}, f32[3,32,256]{2,1,0:T(8,128)S(1)}, u32[]{:S(2)}, u32[]{:S(2)}) collective-permute-start(f32[3,32,256]{2,1,0:T(8,128)S(1)} %slice_bitcast_fusion.17), channel_id=1, source_target_pairs={{0,32},{32,64},{64,96},{96,128},{128,160},{160,192},{192,224},{1,3... | collective-permute-start | bytes 294920 | tf_op jit(solution)/shard_map/ppermute | solution.py:23
  19.4 0.9 copy-start.1
  19.4 1.0 copy-start
  28.4 41.6 %all-to-all-start = ((f32[8,2,6,32,256]{4,3,2,1,0:T(8,128)}), f32[8,2,6,32,256]{4,3,2,1,0:T(8,128)S(1)}, u32[]{:S(2)}, u32[]{:S(2)}) async-start(f32[8,2,6,32,256]{4,3,2,1,0:T(8,128)} %copy.90), calls=%async_computation | async-start | bytes 6291456 | tf_op jit(solution)/shard_map/all_to_all | solution.py:53
  72.2 6.8 %collective-permute-start.5 = (f32[2,2,3,32,6]{4,3,2,1,0:T(8,128)S(1)}, f32[2,2,3,32,6]{4,3,2,1,0:T(8,128)S(1)}, u32[]{:S(2)}, u32[]{:S(2)}) collective-permute-start(f32[2,2,3,32,6]{4,3,2,1,0:T(8,128)S(1)} %get-tuple-element.61), channel_id=1, source_target_pairs={{0,8},{8,16},{16,24},{24,0},{1,9},{9,17},{17,25},{25,1},{2,10},{10... | collective-permute-start | bytes 27656 | tf_op jit(solution)/shard_map/ppermute | solution.py:64
  72.4 6.6 %collective-permute-start.6 = (f32[2,2,3,32,6]{4,3,2,1,0:T(8,128)S(1)}, f32[2,2,3,32,6]{4,3,2,1,0:T(8,128)S(1)}, u32[]{:S(2)}, u32[]{:S(2)}) collective-permute-start(f32[2,2,3,32,6]{4,3,2,1,0:T(8,128)S(1)} %get-tuple-element.62), channel_id=1, source_target_pairs={{8,0},{16,8},{24,16},{0,24},{9,1},{17,9},{25,17},{1,25},{10,2},{18... | collective-permute-start | bytes 27656 | tf_op jit(solution)/shard_map/ppermute | solution.py:65
  79.2 5.3 %collective-permute-start.7 = (f32[2,2,3,6,268]{4,3,2,1,0:T(8,128)S(1)}, f32[2,2,3,6,268]{4,3,2,1,0:T(8,128)S(1)}, u32[]{:S(2)}, u32[]{:S(2)}) collective-permute-start(f32[2,2,3,6,268]{4,3,2,1,0:T(8,128)S(1)} %get-tuple-element.45), channel_id=1, source_target_pairs={{0,1},{1,2},{2,3},{3,4},{4,5},{5,6},{6,7},{7,0},{8,9},{9,10},{10,1... | collective-permute-start | bytes 231560 | tf_op jit(solution)/shard_map/ppermute | solution.py:64
  79.3 5.2 %collective-permute-start.8 = (f32[2,2,3,6,268]{4,3,2,1,0:T(8,128)S(1)}, f32[2,2,3,6,268]{4,3,2,1,0:T(8,128)S(1)}, u32[]{:S(2)}, u32[]{:S(2)}) collective-permute-start(f32[2,2,3,6,268]{4,3,2,1,0:T(8,128)S(1)} %get-tuple-element.46), channel_id=1, source_target_pairs={{1,0},{2,1},{3,2},{4,3},{5,4},{6,5},{7,6},{0,7},{9,8},{10,9},{11,1... | collective-permute-start | bytes 231560 | tf_op jit(solution)/shard_map/ppermute | solution.py:65
  102.7 27.1 %all-to-all-start.1 = ((f32[8,2,3,32,256]{4,3,2,1,0:T(8,128)}), f32[8,2,3,32,256]{4,3,2,1,0:T(8,128)S(1)}, u32[]{:S(2)}, u32[]{:S(2)}) async-start(f32[8,2,3,32,256]{4,3,2,1,0:T(8,128)} %bitcast.135), calls=%async_computation.1 | async-start | bytes 3145728 | tf_op jit(solution)/shard_map/all_to_all | solution.py:53
where the time goes:
time: 131 us
  waiting for transfers between devices  62.9 us (48%)
  starting transfers between devices  29.9 us (23%)
  other arithmetic  16.7 us (13%)
  local copies, waits for them, and re-layouts  14.3 us (11%)
  matrix products  5.79 us (4%)
    all_to_all x2, waiting for transfers between devices, sent_and_summed(): lax.all_to_all(in_blocks(array, dim, count), axis, 0, 0, tiled=True)  56.8 us
    all_to_all x2, starting transfers between devices, sent_and_summed(): lax.all_to_all(in_blocks(array, dim, count), axis, 0, 0, tiled=True)  10.6 us
    ppermute x2, waiting for transfers between devices, with_halo_2(): before = lax.ppermute(last, axis, up)  6.05 us
    add x11, other arithmetic, cheb_turn(): solution = (solution[0] + update[0], solution[1] + update[1])  5.63 us
    ppermute x2, starting transfers between devices, with_halo(): lax.ppermute(first, axis, [(b, a) for a, b in up])  5.56 us
    ppermute x2, starting transfers between devices, with_halo_2(): after = lax.ppermute(first, axis, down)  5.25 us
    ppermute x1, starting transfers between devices, passed_along(): lax.ppermute(value, axis, [(source, source + steps) for source in range(f...  4.36 us
    another operation x14, other arithmetic, wave(): return jnp.stack([height_rate, east_rate, north_rate], axis=-3)  4.29 us
  transfers between devices with their start and end apart: 11, of which 4 were waited for; matrix products, arithmetic and copies ran while one was open for 5% of the time, Pallas kernels for 0%

commit v1 on v0

v1 whole, which is shorter than its diff:
```python
import math

import jax
import jax.numpy as jnp
import numpy as np
from jax import lax
from jax.experimental import pallas as pl
from jax.experimental.pallas import tpu as pltpu
from jax.sharding import PartitionSpec as P

MESH = pl.DeviceIdType.MESH
F32 = jnp.float32

CHEB = 6
STEPS = 16
courant = 1.5
coriolis_mean = 0.3
coriolis_slope = 0.4
circulant = 0.1
spectrum_edge = 5.0

HALO = 8
ROWS = 32
TALL = ROWS + 2 * HALO
WRAPS = 1.0 / circulant


def power_table():
    beta = circulant ** (1.0 / STEPS)
    solved = np.zeros((STEPS, CHEB + 1), complex)
    for k in range(STEPS):
        theta = 2.0 * np.pi * k / STEPS
        shift = 1.0 - beta * np.cos(theta) + 1j * beta * np.sin(theta)
        edge = 1j * spectrum_edge
        sigma = shift / edge
        rho_old = 1.0 / sigma
        one = np.zeros(CHEB + 2, complex)
        one[0] = 1.0
        update = one / shift
        total = update.copy()
        for _ in range(CHEB):
            misfit = one - (shift * total + np.roll(total, 1))
            rho_new = 1.0 / (2.0 * sigma - rho_old)
            update = rho_new * rho_old * update + 2.0 * rho_new / edge * misfit
            total = total + update
            rho_old = rho_new
        solved[k] = total[: CHEB + 1]
    turns = np.exp(2j * np.pi / STEPS * np.outer(np.arange(STEPS), np.arange(STEPS)))
    table = (turns @ solved).real / STEPS
    return table * spectrum_edge ** np.arange(CHEB + 1)


TABLE = power_table()


def weight(delta, p, q, m):
    difference = 2 * delta + p - q
    return float(circulant ** (-difference / STEPS) * TABLE[difference % STEPS, m])


def kernel(
    traj, init, upd_out, res_out,
    state, powers, prev, strip_l, strip_r, edge_l, edge_r, res_buf,
    cross, crossed, own, relay, near_a, near_b, out_buf,
    load_sem, halo_s, halo_r, cross_s, cross_r, ring_s, ring_r, store_sem,
):
    tm, gx, gy = lax.axis_index("tm"), lax.axis_index("gx"), lax.axis_index("gy")
    n_tm, n_gx, n_gy = lax.axis_size("tm"), lax.axis_size("gx"), lax.axis_size("gy")
    core = lax.rem(tm, 2)
    east, west = lax.rem(gx + 1, n_gx), lax.rem(gx + n_gx - 1, n_gx)
    north, south = lax.rem(gy + 1, n_gy), lax.rem(gy + n_gy - 1, n_gy)
    after, before = lax.rem(tm + 1, n_tm), lax.rem(tm + n_tm - 1, n_tm)
    chip_up, chip_down = lax.rem(tm + 2, n_tm), lax.rem(tm + n_tm - 2, n_tm)
    partner = tm + 1 - 2 * core
    last = tm == n_tm - 1

    loads = []
    for lane in range(2):
        columns = pl.ds(128 * lane, 128)
        loads.append(pltpu.make_async_copy(
            traj.at[:, :, :, columns], state.at[pl.ds(0, 2), :, lane, pl.ds(HALO, ROWS), :], load_sem.at[2 * lane]))
        loads.append(pltpu.make_async_copy(
            init.at[:, :, columns], state.at[2, :, lane, pl.ds(HALO, ROWS), :], load_sem.at[2 * lane + 1]))
    for load in loads:
        load.start()

    around = [(tm, west, gy), (tm, east, gy), (tm, gx, south), (tm, gx, north),
              (tm, west, south), (tm, west, north), (tm, east, south), (tm, east, north)]
    peers = around + [(partner, gx, gy), (chip_up, gx, gy), (chip_down, gx, gy),
                      (jnp.where(core == 1, after, before), gx, gy)]
    barrier = pltpu.get_barrier_semaphore()
    for peer in peers:
        pl.semaphore_signal(barrier, inc=1, device_id=peer, device_id_type=MESH)

    for load in loads:
        load.wait()

    lane_id = lax.broadcasted_iota(jnp.int32, (TALL, 128), 1)
    packed_l = jnp.zeros((ROWS, 128), F32)
    packed_r = jnp.zeros((ROWS, 128), F32)
    for s in range(3):
        for f in range(3):
            spot = 8 * (3 * s + f)
            here = (lane_id[:ROWS] >= spot) & (lane_id[:ROWS] < spot + 8)
            left = state[s, f, 0, pl.ds(HALO, ROWS), :]
            right = state[s, f, 1, pl.ds(HALO, ROWS), :]
            packed_l = jnp.where(here, pltpu.roll(left, spot, 1) if spot else left, packed_l)
            packed_r = jnp.where(here, pltpu.roll(right, spot + 8, 1), packed_r)
    strip_l[...] = packed_l
    strip_r[...] = packed_r

    pl.semaphore_wait(barrier, len(peers))

    def remote(src, dst, send, recv, peer):
        return pltpu.make_async_remote_copy(
            src_ref=src, dst_ref=dst, send_sem=send, recv_sem=recv, device_id=peer, device_id_type=MESH)

    top, bottom, low, high = pl.ds(0, HALO), pl.ds(ROWS - HALO, HALO), pl.ds(HALO, HALO), pl.ds(ROWS, HALO)
    under, over = pl.ds(0, HALO), pl.ds(HALO + ROWS, HALO)
    both, cols = pl.ds(0, 2), pl.ds(0, 2)
    halo = [
        remote(strip_l.at[top], edge_r.at[over], halo_s.at[0], halo_r.at[0], (tm, west, south)),
        remote(strip_l.at[bottom], edge_r.at[under], halo_s.at[1], halo_r.at[1], (tm, west, north)),
        remote(strip_r.at[top], edge_l.at[over], halo_s.at[2], halo_r.at[2], (tm, east, south)),
        remote(strip_r.at[bottom], edge_l.at[under], halo_s.at[3], halo_r.at[3], (tm, east, north)),
        remote(strip_l, edge_r.at[pl.ds(HALO, ROWS)], halo_s.at[4], halo_r.at[4], (tm, west, gy)),
        remote(strip_r, edge_l.at[pl.ds(HALO, ROWS)], halo_s.at[5], halo_r.at[5], (tm, east, gy)),
        remote(state.at[both, :, cols, low, :], state.at[both, :, cols, over, :], halo_s.at[6], halo_r.at[6],
               (tm, gx, south)),
        remote(state.at[both, :, cols, high, :], state.at[both, :, cols, under, :], halo_s.at[7], halo_r.at[7],
               (tm, gx, north)),
    ]
    opening = [
        remote(state.at[2, :, cols, low, :], state.at[2, :, cols, over, :], halo_s.at[8], halo_r.at[8], (tm, gx, south)),
        remote(state.at[2, :, cols, high, :], state.at[2, :, cols, under, :], halo_s.at[9], halo_r.at[9],
               (tm, gx, north)),
    ]
    passed = remote(state.at[1, :, cols, pl.ds(HALO, ROWS), :], prev, halo_s.at[10], halo_r.at[10], (after, gx, gy))
    for copy in halo:
        copy.start()

    @pl.when(last)
    def _():
        for copy in opening:
            copy.start()

    passed.start()

    for copy in halo:
        copy.wait_recv()

    @pl.when(last)
    def _():
        for copy in opening:
            copy.wait_recv()

    for s in range(3):
        for f in range(3):
            spot = 8 * (3 * s + f)
            right = pltpu.roll(edge_r[...], (128 - spot) % 128, 1) if spot else edge_r[...]
            left = pltpu.roll(edge_l[...], 120 - spot, 1)
            state[s, f, 2, :, :] = jnp.where(lane_id < 64, right, left)

    row = (gy * ROWS - HALO + n_gy * ROWS + lax.broadcasted_iota(jnp.int32, (TALL, 128), 0)) % (n_gy * ROWS)
    rotation = coriolis_mean + coriolis_slope * ((row.astype(F32) + 0.5) / (n_gy * ROWS) - 0.5)

    first_lane, final_lane = lane_id == 0, lane_id == 127

    def dx(tiles):
        ahead = [pltpu.roll(t, 127, 1) for t in tiles]
        behind = [pltpu.roll(t, 1, 1) for t in tiles]
        return [jnp.where(final_lane, ahead[(l + 1) % 3], ahead[l]) - jnp.where(first_lane, behind[(l + 2) % 3], behind[l])
                for l in range(3)]

    def dy(tile):
        return pltpu.roll(tile, TALL - 1, 0) - pltpu.roll(tile, 1, 0)

    def start_fields(s, carry):
        h = [state[s, 0, l, :, :] for l in range(3)]
        u = [state[s, 1, l, :, :] for l in range(3)]
        v = [state[s, 2, l, :, :] for l in range(3)]
        flux = dx([u[l] + h[l] * u[l] for l in range(3)])
        slope_h, slope_u, slope_v = dx(h), dx(u), dx(v)
        for l in range(3):
            powers[0, s, 0, l, :, :] = h[l] + courant * (flux[l] + dy(v[l] + h[l] * v[l]))
            powers[0, s, 1, l, :, :] = u[l] + (
                courant * slope_h[l] - rotation * v[l] + courant * (u[l] * slope_u[l] + v[l] * dy(u[l])))
            powers[0, s, 2, l, :, :] = v[l] + (
                courant * dy(h[l]) + rotation * u[l] + courant * (u[l] * slope_v[l] + v[l] * dy(v[l])))
        return carry

    lax.fori_loop(0, 2, start_fields, 0)

    slot = jnp.where(last, 2, 1)
    factor = jnp.where(last, -WRAPS, -1.0).astype(F32)
    for f in range(3):
        for l in range(3):
            powers[0, 2, f, l, :, :] = factor * state[slot, f, l, :, :]
            powers[0, 1, f, l, :, :] = powers[0, 1, f, l, :, :] - state[0, f, l, :, :]

    step = courant / spectrum_edge
    turning = rotation * (1.0 / spectrum_edge)

    def next_power(m, carry):
        for q in range(3):
            h = [powers[m, q, 0, l, :, :] for l in range(3)]
            u = [powers[m, q, 1, l, :, :] for l in range(3)]
            v = [powers[m, q, 2, l, :, :] for l in range(3)]
            slope_h, slope_u = dx(h), dx(u)
            for l in range(3):
                powers[m + 1, q, 0, l, :, :] = step * (slope_u[l] + dy(v[l]))
                powers[m + 1, q, 1, l, :, :] = step * slope_h[l] - turning * v[l]
                powers[m + 1, q, 2, l, :, :] = step * dy(h[l]) + turning * u[l]
        return carry

    lax.fori_loop(0, CHEB, next_power, 0)

    PIECE = 16
    pieces = ROWS // PIECE

    def mix(f, wanted):
        def body(i, carry):
            l, t = i // pieces, i % pieces
            source = pl.ds(pl.multiple_of(HALO + PIECE * t, 8), PIECE)
            rows = pl.ds(pl.multiple_of(PIECE * t, 8), PIECE)
            terms = [[powers[m, q, f, l, source, :] for m in range(CHEB + 1)] for q in range(3)]
            for delta, p, store in wanted:
                total = None
                for q in range(3):
                    for m in range(CHEB + 1):
                        term = weight(delta, p, q, m) * terms[q][m]
                        total = term if total is None else total + term
                if delta:
                    total = total * jnp.where(tm + delta >= n_tm, circulant, 1.0).astype(F32)
                store(l, rows, total)
            return carry
        lax.fori_loop(0, 2 * pieces, body, 0)

    def into(ref, *index):
        def store(l, rows, value):
            ref[(*index, l, rows, slice(None))] = value
        return store

    def cross_copy(odd, f):
        where = lax.rem(odd + core, 4)
        return remote(cross.at[odd, f], crossed.at[where, f], cross_s.at[odd, f], cross_r.at[where, f],
                      (partner, gx, gy))

    def crossed_in(place, f):
        return remote(cross.at[place, f], crossed.at[place, f], cross_s.at[place, f], cross_r.at[place, f],
                      (partner, gx, gy))

    up, down = (chip_up, gx, gy), (chip_down, gx, gy)

    def ring_copy(stage, side, src, dst, f):
        return remote(src, dst, ring_s.at[stage, side, f], ring_r.at[stage, side, f], down if side else up)

    def far_copy(side, f):
        return ring_copy(0, side, own.at[0, f, side], relay.at[side, f], f)

    def near_copy(side, f):
        return ring_copy(1, side, own.at[1 + side, f, 1 - side], near_a.at[side, f], f)

    def relayed_copy(side, f):
        return ring_copy(2, side, own.at[1 + side, f, side], near_b.at[side, f], f)

    def m1(f, carry):
        mix(f, [(3, 0, into(cross, 1, f, 0)), (3, 1, into(cross, 1, f, 1)),
                (5, 0, into(cross, 2, f, 0)), (5, 1, into(cross, 2, f, 1))])
        cross_copy(1, f).start()
        cross_copy(2, f).start()
        return carry

    def m2(f, carry):
        mix(f, [(4, 0, into(own, 0, f, 0)), (4, 1, into(own, 0, f, 1))])
        return carry

    def s1(f, carry):
        crossed_in(2, f).wait_recv()
        own[0, f] = own[0, f] + crossed[2, f]
        far_copy(0, f).start()
        far_copy(1, f).start()
        return carry

    def m3(f, carry):
        mix(f, [(1, 0, into(cross, 0, f, 0)), (1, 1, into(cross, 0, f, 1)),
                (7, 0, into(cross, 3, f, 0)), (7, 1, into(cross, 3, f, 1))])
        cross_copy(0, f).start()
        cross_copy(3, f).start()
        return carry

    def m4(f, carry):
        mix(f, [(2, 0, into(own, 1, f, 0)), (2, 1, into(own, 1, f, 1)),
                (6, 0, into(own, 2, f, 0)), (6, 1, into(own, 2, f, 1))])
        return carry

    def s2(f, carry):
        crossed_in(1, f).wait_recv()
        crossed_in(3, f).wait_recv()
        own[1, f] = own[1, f] + crossed[1, f]
        own[2, f] = own[2, f] + crossed[3, f]
        near_copy(0, f).start()
        near_copy(1, f).start()
        return carry

    def s3(f, carry):
        for side in range(2):
            far_copy(side, f).wait_recv()
            own[1 + side, f, side] = own[1 + side, f, side] + relay[side, f]
            relayed_copy(side, f).start()
        return carry

    def m5(f, carry):
        mix(f, [(0, 0, into(own, 3, f, 0)), (0, 1, into(own, 3, f, 1))])
        crossed_in(0, f).wait_recv()
        for p in range(2):
            for l in range(2):
                out_buf[p, f, l] = state[p, f, l, pl.ds(HALO, ROWS), :] - (own[3, f, p, l] + crossed[0, f, p, l])
        return carry

    lax.fori_loop(0, 3, m1, 0)
    lax.fori_loop(0, 3, m2, 0)
    lax.fori_loop(0, 3, s1, 0)
    lax.fori_loop(0, 3, m3, 0)
    lax.fori_loop(0, 3, m4, 0)
    lax.fori_loop(0, 3, s2, 0)
    lax.fori_loop(0, 3, s3, 0)
    lax.fori_loop(0, 3, m5, 0)

    passed.wait_recv()
    for f in range(3):
        for l in range(2):
            before_first = jnp.where(tm == 0, state[2, f, l, pl.ds(HALO, ROWS), :], prev[f, l])
            res_buf[0, f, l] = powers[0, 0, f, l, pl.ds(HALO, ROWS), :] - before_first
            res_buf[1, f, l] = powers[0, 1, f, l, pl.ds(HALO, ROWS), :]
    stores = [pltpu.make_async_copy(res_buf.at[:, :, l], res_out.at[:, :, :, pl.ds(128 * l, 128)], store_sem.at[l])
              for l in range(2)]
    for store in stores:
        store.start()

    def finish(f, carry):
        for side in range(2):
            near_copy(side, f).wait_recv()
            relayed_copy(side, f).wait_recv()
        for l in range(2):
            out_buf[0, f, l] = out_buf[0, f, l] - (near_b[0, f, l] + near_a[1, f, l])
            out_buf[1, f, l] = out_buf[1, f, l] - (near_a[0, f, l] + near_b[1, f, l])
        return carry

    lax.fori_loop(0, 3, finish, 0)
    ends = [pltpu.make_async_copy(out_buf.at[:, :, l], upd_out.at[:, :, :, pl.ds(128 * l, 128)], store_sem.at[2 + l])
            for l in range(2)]
    for end in ends:
        end.start()

    for copy in halo:
        copy.wait_send()

    @pl.when(last)
    def _():
        for copy in opening:
            copy.wait_send()

    passed.wait_send()

    def drain(f, carry):
        for odd in range(4):
            cross_copy(odd, f).wait_send()
        for side in range(2):
            far_copy(side, f).wait_send()
            near_copy(side, f).wait_send()
            relayed_copy(side, f).wait_send()
        return carry

    lax.fori_loop(0, 3, drain, 0)
    for store in stores + ends:
        store.wait()


def shards(trajectory, initial):
    whole = jax.ShapeDtypeStruct(trajectory.shape, F32)
    anywhere = pl.BlockSpec(memory_space=pl.ANY)
    dma = pltpu.SemaphoreType.DMA
    return pl.pallas_call(
        kernel,
        out_shape=(whole, whole),
        in_specs=[anywhere, anywhere],
        out_specs=(anywhere, anywhere),
        scratch_shapes=[
            pltpu.VMEM((3, 3, 3, TALL, 128), F32),
            pltpu.VMEM((CHEB + 1, 3, 3, 3, TALL, 128), F32),
            pltpu.VMEM((3, 2, ROWS, 128), F32),
            pltpu.VMEM((ROWS, 128), F32),
            pltpu.VMEM((ROWS, 128), F32),
            pltpu.VMEM((TALL, 128), F32),
            pltpu.VMEM((TALL, 128), F32),
            pltpu.VMEM((2, 3, 2, ROWS, 128), F32),
            pltpu.VMEM((4, 3, 2, 2, ROWS, 128), F32),
            pltpu.VMEM((4, 3, 2, 2, ROWS, 128), F32),
            pltpu.VMEM((4, 3, 2, 2, ROWS, 128), F32),
            pltpu.VMEM((2, 3, 2, ROWS, 128), F32),
            pltpu.VMEM((2, 3, 2, ROWS, 128), F32),
            pltpu.VMEM((2, 3, 2, ROWS, 128), F32),
            pltpu.VMEM((2, 3, 2, ROWS, 128), F32),
            dma((4,)),
            dma((11,)),
            dma((11,)),
            dma((4, 3)),
            dma((4, 3)),
            dma((3, 2, 3)),
            dma((3, 2, 3)),
            dma((4,)),
        ],
        compiler_params=pltpu.CompilerParams(collective_id=0, has_side_effects=True),
        name="paradiag",
    )(trajectory, initial)


def solution(mesh):
    in_specs = (P("tm", None, "gy", "gx"), P(None, "gy", "gx"))
    out_specs = (P("tm", None, "gy", "gx"), P("tm", None, "gy", "gx"))
    return jax.shard_map(shards, mesh=mesh, in_specs=in_specs, out_specs=out_specs, check_vma=False)
```

time: 131 us -> 31.7 us (0.24)
  waiting for transfers between devices: 62.9 us -> 0 us
  starting transfers between devices: 29.9 us -> 0 us
  Pallas kernels: 0 us -> 28.5 us
  other arithmetic: 16.7 us -> 0 us
  local copies, waits for them, and re-layouts: 14.3 us -> 2.34 us
  matrix products: 5.79 us -> 0 us
    all_to_all x2 -> x0, waiting for transfers between devices: 56.8 us -> none  [sent_and_summed(): lax.all_to_all(in_blocks(array, dim, count), axis, 0, 0, tiled=True)]
    pallas_call x0 -> x1, Pallas kernels: none -> 28.5 us  [shards(): pl.pallas_call(kernel, out_shape=(whole, whole), in_specs=[anywhere, anyw...]
    ppermute x9 -> x0, starting transfers between devices: 19.3 us -> none  [the longest x2 5.56 us: with_halo(): lax.ppermute(first, axis, [(b, a) for a, b in up])]
    all_to_all x2 -> x0, starting transfers between devices: 10.6 us -> none  [sent_and_summed(): lax.all_to_all(in_blocks(array, dim, count), axis, 0, 0, tiled=True)]
    add x21 -> x0, other arithmetic: 6.26 us -> none  [the longest x11 5.63 us: cheb_turn(): solution = (solution[0] + update[0], solution[1] + update[1])]
    ppermute x9 -> x0, waiting for transfers between devices: 6.07 us -> none  [the longest x2 6.05 us: with_halo_2(): before = lax.ppermute(last, axis, up)]
    slice x16 -> x0, local copies, waits for them, and re-layouts: 5.82 us -> none  [the longest x6 2.42 us: crop_cycle(): values[..., margin:values.shape[-2] - margin, margin:values.shape[-1] - m...]
    dot_general x4 -> x0, matrix products: 5.79 us -> none  [the longest x1 1.54 us: shards(): jnp.dot(jnp.cos(table), whole_local, precision=highest)]
  transfers between devices with their start and end apart: 11 -> 0, of which waited for: 4 -> 0; matrix products, arithmetic and copies ran while one was open for 5% -> 0% of each run, Pallas kernels for 0% -> 0%
where the time goes in v1:
time: 31.7 us; the launch traced here: 31.5 us
  Pallas kernels  28.5 us (90%)
  local copies, waits for them, and re-layouts  2.34 us (7%)
  between operations  0.65 us (2%)
    pallas_call x1, Pallas kernels, shards(): pl.pallas_call(kernel, out_shape=(whole, whole), in_specs=[anywhere, anyw...  28.5 us
    unnamed x4, local copies, waits for them, and re-layouts  2.34 us

profile of v1, /device:TPU:1, one launch (start us, length us, event | category | flops | bytes accessed | tf_op | source)
XLA Modules:
  0.0 31.5 jit_solution(1929151291159215265)
XLA Ops:
  0.6 28.5 %paradiag.1 = (f32[2,3,32,256]{3,2,1,0:T(8,128)}, f32[2,3,32,256]{3,2,1,0:T(8,128)}) custom-call(f32[2,3,32,256]{3,2,1,0:T(8,128)} %traj.1, f32[3,32,256]{2,1,0:T(8,128)} %init.1), custom_call_target="tpu_custom_call" | custom-call | tf_op jit(solution)/shard_map/paradiag/pallas_call | solution.py:384
  29.2 0.0 copy-start
  29.2 1.7 %copy.6 = f32[2,3,32,256]{3,2,1,0:T(8,128)} copy(f32[2,3,32,256]{3,2,1,0:T(8,128)} %get-tuple-element.4) | data formatting | bytes 393216
  30.8 0.0 copy-done
  30.8 0.7 %copy.7 = f32[2,3,32,256]{3,2,1,0:T(8,128)} copy(f32[2,3,32,256]{3,2,1,0:T(8,128)S(1)} %copy-done) | data formatting | bytes 393216
Async XLA Ops:
  29.2 1.7 %copy-start = (f32[2,3,32,256]{3,2,1,0:T(8,128)S(1)}, f32[2,3,32,256]{3,2,1,0:T(8,128)}, u32[]{:S(2)}) copy-start(f32[2,3,32,256]{3,2,1,0:T(8,128)} %get-tuple-element.5) | copy-start | bytes 589828

commit v2 on v1

--- a/solution.py
+++ b/solution.py
@@ -22,7 +22,11 @@
 HALO = 8
 ROWS = 32
 TALL = ROWS + 2 * HALO
+EDGE = 8
+BASE = EDGE + HALO
+DEEP = TALL + 2 * EDGE
 WRAPS = 1.0 / circulant
+OPPOSITE = (1, 0, 3, 2, 5, 4, 7, 6, 8, 10, 9, 11)
 
 
 def power_table():
@@ -47,7 +51,7 @@
         solved[k] = total[: CHEB + 1]
     turns = np.exp(2j * np.pi / STEPS * np.outer(np.arange(STEPS), np.arange(STEPS)))
     table = (turns @ solved).real / STEPS
-    return table * spectrum_edge ** np.arange(CHEB + 1)
+    return table * courant ** np.arange(CHEB + 1)
 
 
 TABLE = power_table()
@@ -59,10 +63,10 @@
 
 
 def kernel(
-    traj, init, upd_out, res_out,
-    state, powers, prev, strip_l, strip_r, edge_l, edge_r, res_buf,
-    cross, crossed, own, relay, near_a, near_b, out_buf,
-    load_sem, halo_s, halo_r, cross_s, cross_r, ring_s, ring_r, store_sem,
+    traj, init, out_buf, res_buf,
+    state, powers, rotation, prev, strip_l, strip_r, edge_l, edge_r,
+    cross, crossed, own, relay, near_a, near_b,
+    ready, load_sem, halo_s, halo_r, cross_s, cross_r, ring_s, ring_r,
 ):
     tm, gx, gy = lax.axis_index("tm"), lax.axis_index("gx"), lax.axis_index("gy")
     n_tm, n_gx, n_gy = lax.axis_size("tm"), lax.axis_size("gx"), lax.axis_size("gy")
@@ -78,19 +82,47 @@
     for lane in range(2):
         columns = pl.ds(128 * lane, 128)
         loads.append(pltpu.make_async_copy(
-            traj.at[:, :, :, columns], state.at[pl.ds(0, 2), :, lane, pl.ds(HALO, ROWS), :], load_sem.at[2 * lane]))
+            traj.at[:, :, :, columns], state.at[pl.ds(0, 2), :, lane, pl.ds(BASE, ROWS), :], load_sem.at[2 * lane]))
         loads.append(pltpu.make_async_copy(
-            init.at[:, :, columns], state.at[2, :, lane, pl.ds(HALO, ROWS), :], load_sem.at[2 * lane + 1]))
+            init.at[:, :, columns], state.at[2, :, lane, pl.ds(BASE, ROWS), :], load_sem.at[2 * lane + 1]))
     for load in loads:
         load.start()
 
-    around = [(tm, west, gy), (tm, east, gy), (tm, gx, south), (tm, gx, north),
-              (tm, west, south), (tm, west, north), (tm, east, south), (tm, east, north)]
-    peers = around + [(partner, gx, gy), (chip_up, gx, gy), (chip_down, gx, gy),
-                      (jnp.where(core == 1, after, before), gx, gy)]
+    def arrival(t, x, y):
+        chip, seat = t // 2, t % 2
+        by_x = chip + (chip + 3) // 4
+        by_y = x + x // 2 - 2 * (x // 3)
+        by_z = jnp.minimum(2 * y, 66 - 9 * y)
+        return ((by_x + by_y + by_z) * 2 + 1 - seat) * 256 + t * 32 + x * 8 + y
+
+    across = jnp.where(core == 1, after, before)
+    peers = [(tm, east, gy), (tm, west, gy), (tm, gx, north), (tm, gx, south),
+             (tm, east, north), (tm, west, south), (tm, east, south), (tm, west, north),
+             (partner, gx, gy), (chip_up, gx, gy), (chip_down, gx, gy), (across, gx, gy)]
+    mine = arrival(tm, gx, gy)
+    earlier = [(arrival(*peer) < mine).astype(jnp.int32) for peer in peers]
+
     barrier = pltpu.get_barrier_semaphore()
-    for peer in peers:
-        pl.semaphore_signal(barrier, inc=1, device_id=peer, device_id_type=MESH)
+    for peer, sooner in zip(peers, earlier, strict=True):
+        @pl.when(sooner == 0)
+        def _(peer=peer):
+            pl.semaphore_signal(barrier, inc=1, device_id=peer, device_id_type=MESH)
+
+    sooner_count = sum(earlier)
+
+    @pl.when(sooner_count > 0)
+    def _():
+        pl.semaphore_wait(barrier, sooner_count)
+
+    for i, (peer, sooner) in enumerate(zip(peers, earlier, strict=True)):
+        @pl.when(sooner == 1)
+        def _(i=i, peer=peer):
+            pl.semaphore_signal(ready.at[OPPOSITE[i]], inc=1, device_id=peer, device_id_type=MESH)
+
+    def met(i):
+        @pl.when(earlier[i] == 0)
+        def _():
+            pl.semaphore_wait(ready.at[i], 1)
 
     for load in loads:
         load.wait()
@@ -102,51 +134,68 @@
         for f in range(3):
             spot = 8 * (3 * s + f)
             here = (lane_id[:ROWS] >= spot) & (lane_id[:ROWS] < spot + 8)
-            left = state[s, f, 0, pl.ds(HALO, ROWS), :]
-            right = state[s, f, 1, pl.ds(HALO, ROWS), :]
+            left = state[s, f, 0, pl.ds(BASE, ROWS), :]
+            right = state[s, f, 1, pl.ds(BASE, ROWS), :]
             packed_l = jnp.where(here, pltpu.roll(left, spot, 1) if spot else left, packed_l)
             packed_r = jnp.where(here, pltpu.roll(right, spot + 8, 1), packed_r)
     strip_l[...] = packed_l
     strip_r[...] = packed_r
 
-    pl.semaphore_wait(barrier, len(peers))
-
     def remote(src, dst, send, recv, peer):
         return pltpu.make_async_remote_copy(
             src_ref=src, dst_ref=dst, send_sem=send, recv_sem=recv, device_id=peer, device_id_type=MESH)
 
-    top, bottom, low, high = pl.ds(0, HALO), pl.ds(ROWS - HALO, HALO), pl.ds(HALO, HALO), pl.ds(ROWS, HALO)
-    under, over = pl.ds(0, HALO), pl.ds(HALO + ROWS, HALO)
+    top, bottom, low, high = pl.ds(0, HALO), pl.ds(ROWS - HALO, HALO), pl.ds(BASE, HALO), pl.ds(EDGE + ROWS, HALO)
+    first, final = pl.ds(0, HALO), pl.ds(HALO + ROWS, HALO)
+    under, over = pl.ds(EDGE, HALO), pl.ds(BASE + ROWS, HALO)
     both, cols = pl.ds(0, 2), pl.ds(0, 2)
-    halo = [
-        remote(strip_l.at[top], edge_r.at[over], halo_s.at[0], halo_r.at[0], (tm, west, south)),
-        remote(strip_l.at[bottom], edge_r.at[under], halo_s.at[1], halo_r.at[1], (tm, west, north)),
-        remote(strip_r.at[top], edge_l.at[over], halo_s.at[2], halo_r.at[2], (tm, east, south)),
-        remote(strip_r.at[bottom], edge_l.at[under], halo_s.at[3], halo_r.at[3], (tm, east, north)),
-        remote(strip_l, edge_r.at[pl.ds(HALO, ROWS)], halo_s.at[4], halo_r.at[4], (tm, west, gy)),
-        remote(strip_r, edge_l.at[pl.ds(HALO, ROWS)], halo_s.at[5], halo_r.at[5], (tm, east, gy)),
-        remote(state.at[both, :, cols, low, :], state.at[both, :, cols, over, :], halo_s.at[6], halo_r.at[6],
-               (tm, gx, south)),
-        remote(state.at[both, :, cols, high, :], state.at[both, :, cols, under, :], halo_s.at[7], halo_r.at[7],
+    def halo_copy(i, src, dst):
+        return remote(src, dst, halo_s.at[i], halo_r.at[OPPOSITE[i]], peers[i])
+
+    def halo_in(i, src, dst):
+        return remote(src, dst, halo_s.at[i], halo_r.at[i], peers[i])
+
+    middle = pl.ds(HALO, ROWS)
+    sides = [
+        (strip_r, edge_l.at[middle], strip_l, edge_r.at[middle]),
+        (strip_l, edge_r.at[middle], strip_r, edge_l.at[middle]),
+        (state.at[both, :, cols, high, :], state.at[both, :, cols, under, :],
+         state.at[both, :, cols, low, :], state.at[both, :, cols, over, :]),
+        (state.at[both, :, cols, low, :], state.at[both, :, cols, over, :],
+         state.at[both, :, cols, high, :], state.at[both, :, cols, under, :]),
+        (strip_r.at[bottom], edge_l.at[first], strip_l.at[top], edge_r.at[final]),
+        (strip_l.at[top], edge_r.at[final], strip_r.at[bottom], edge_l.at[first]),
+        (strip_r.at[top], edge_l.at[final], strip_l.at[bottom], edge_r.at[first]),
+        (strip_l.at[bottom], edge_r.at[first], strip_r.at[top], edge_l.at[final]),
+    ]
+    halo = [halo_copy(i, sides[i][0], sides[i][1]) for i in range(8)]
+    arriving = [halo_in(i, sides[i][2], sides[i][3]) for i in range(8)]
+    opening = [
+        remote(state.at[2, :, cols, high, :], state.at[2, :, cols, under, :], halo_s.at[8], halo_r.at[8],
                (tm, gx, north)),
+        remote(state.at[2, :, cols, low, :], state.at[2, :, cols, over, :], halo_s.at[9], halo_r.at[9], (tm, gx, south)),
     ]
-    opening = [
-        remote(state.at[2, :, cols, low, :], state.at[2, :, cols, over, :], halo_s.at[8], halo_r.at[8], (tm, gx, south)),
-        remote(state.at[2, :, cols, high, :], state.at[2, :, cols, under, :], halo_s.at[9], halo_r.at[9],
-               (tm, gx, north)),
-    ]
-    passed = remote(state.at[1, :, cols, pl.ds(HALO, ROWS), :], prev, halo_s.at[10], halo_r.at[10], (after, gx, gy))
-    for copy in halo:
-        copy.start()
+    passed = remote(state.at[1, :, cols, pl.ds(BASE, ROWS), :], prev, halo_s.at[10], halo_r.at[10], (after, gx, gy))
+    for i in range(8):
+        @pl.when(earlier[i] == 1)
+        def _(i=i):
+            halo[i].start()
+    for i in range(8):
+        @pl.when(earlier[i] == 0)
+        def _(i=i):
+            pl.semaphore_wait(ready.at[i], 1)
+            halo[i].start()
 
     @pl.when(last)
     def _():
         for copy in opening:
             copy.start()
 
+    for i in range(8, 12):
+        met(i)
     passed.start()
 
-    for copy in halo:
+    for copy in arriving:
         copy.wait_recv()
 
     @pl.when(last)
@@ -154,15 +203,17 @@
         for copy in opening:
             copy.wait_recv()
 
+    tall = pl.ds(EDGE, TALL)
     for s in range(3):
         for f in range(3):
             spot = 8 * (3 * s + f)
             right = pltpu.roll(edge_r[...], (128 - spot) % 128, 1) if spot else edge_r[...]
             left = pltpu.roll(edge_l[...], 120 - spot, 1)
-            state[s, f, 2, :, :] = jnp.where(lane_id < 64, right, left)
+            state[s, f, 2, tall, :] = jnp.where(lane_id < 64, right, left)
 
     row = (gy * ROWS - HALO + n_gy * ROWS + lax.broadcasted_iota(jnp.int32, (TALL, 128), 0)) % (n_gy * ROWS)
-    rotation = coriolis_mean + coriolis_slope * ((row.astype(F32) + 0.5) / (n_gy * ROWS) - 0.5)
+    latitude = coriolis_mean + coriolis_slope * ((row.astype(F32) + 0.5) / (n_gy * ROWS) - 0.5)
+    rotation[...] = latitude * (1.0 / courant)
 
     first_lane, final_lane = lane_id == 0, lane_id == 127
 
@@ -172,21 +223,22 @@
         return [jnp.where(final_lane, ahead[(l + 1) % 3], ahead[l]) - jnp.where(first_lane, behind[(l + 2) % 3], behind[l])
                 for l in range(3)]
 
-    def dy(tile):
-        return pltpu.roll(tile, TALL - 1, 0) - pltpu.roll(tile, 1, 0)
+    above, below = pl.ds(EDGE + 1, TALL), pl.ds(EDGE - 1, TALL)
 
     def start_fields(s, carry):
-        h = [state[s, 0, l, :, :] for l in range(3)]
-        u = [state[s, 1, l, :, :] for l in range(3)]
-        v = [state[s, 2, l, :, :] for l in range(3)]
+        h = [state[s, 0, l, tall, :] for l in range(3)]
+        u = [state[s, 1, l, tall, :] for l in range(3)]
+        v = [state[s, 2, l, tall, :] for l in range(3)]
+        turn = rotation[...]
         flux = dx([u[l] + h[l] * u[l] for l in range(3)])
         slope_h, slope_u, slope_v = dx(h), dx(u), dx(v)
         for l in range(3):
-            powers[0, s, 0, l, :, :] = h[l] + courant * (flux[l] + dy(v[l] + h[l] * v[l]))
-            powers[0, s, 1, l, :, :] = u[l] + (
-                courant * slope_h[l] - rotation * v[l] + courant * (u[l] * slope_u[l] + v[l] * dy(u[l])))
-            powers[0, s, 2, l, :, :] = v[l] + (
-                courant * dy(h[l]) + rotation * u[l] + courant * (u[l] * slope_v[l] + v[l] * dy(v[l])))
+            (ha, hb), (ua, ub), (va, vb) = [(state[s, f, l, above, :], state[s, f, l, below, :]) for f in range(3)]
+            powers[0, s, 0, l, tall, :] = h[l] + courant * (flux[l] + ((va + ha * va) - (vb + hb * vb)))
+            powers[0, s, 1, l, tall, :] = u[l] + courant * (
+                slope_h[l] - turn * v[l] + (u[l] * slope_u[l] + v[l] * (ua - ub)))
+            powers[0, s, 2, l, tall, :] = v[l] + courant * (
+                (ha - hb) + turn * u[l] + (u[l] * slope_v[l] + v[l] * (va - vb)))
         return carry
 
     lax.fori_loop(0, 2, start_fields, 0)
@@ -195,22 +247,22 @@
     factor = jnp.where(last, -WRAPS, -1.0).astype(F32)
     for f in range(3):
         for l in range(3):
-            powers[0, 2, f, l, :, :] = factor * state[slot, f, l, :, :]
-            powers[0, 1, f, l, :, :] = powers[0, 1, f, l, :, :] - state[0, f, l, :, :]
-
-    step = courant / spectrum_edge
-    turning = rotation * (1.0 / spectrum_edge)
+            powers[0, 2, f, l, tall, :] = factor * state[slot, f, l, tall, :]
+            powers[0, 1, f, l, tall, :] = powers[0, 1, f, l, tall, :] - state[0, f, l, tall, :]
 
     def next_power(m, carry):
         for q in range(3):
-            h = [powers[m, q, 0, l, :, :] for l in range(3)]
-            u = [powers[m, q, 1, l, :, :] for l in range(3)]
-            v = [powers[m, q, 2, l, :, :] for l in range(3)]
+            h = [powers[m, q, 0, l, tall, :] for l in range(3)]
+            u = [powers[m, q, 1, l, tall, :] for l in range(3)]
             slope_h, slope_u = dx(h), dx(u)
+            turn = rotation[...]
             for l in range(3):
-                powers[m + 1, q, 0, l, :, :] = step * (slope_u[l] + dy(v[l]))
-                powers[m + 1, q, 1, l, :, :] = step * slope_h[l] - turning * v[l]
-                powers[m + 1, q, 2, l, :, :] = step * dy(h[l]) + turning * u[l]
+                ha, hb = powers[m, q, 0, l, above, :], powers[m, q, 0, l, below, :]
+                va, vb = powers[m, q, 2, l, above, :], powers[m, q, 2, l, below, :]
+                v = powers[m, q, 2, l, tall, :]
+                powers[m + 1, q, 0, l, tall, :] = slope_u[l] + (va - vb)
+                powers[m + 1, q, 1, l, tall, :] = slope_h[l] - turn * v
+                powers[m + 1, q, 2, l, tall, :] = (ha - hb) + turn * u[l]
         return carry
 
     lax.fori_loop(0, CHEB, next_power, 0)
@@ -221,7 +273,7 @@
     def mix(f, wanted):
         def body(i, carry):
             l, t = i // pieces, i % pieces
-            source = pl.ds(pl.multiple_of(HALO + PIECE * t, 8), PIECE)
+            source = pl.ds(pl.multiple_of(BASE + PIECE * t, 8), PIECE)
             rows = pl.ds(pl.multiple_of(PIECE * t, 8), PIECE)
             terms = [[powers[m, q, f, l, source, :] for m in range(CHEB + 1)] for q in range(3)]
             for delta, p, store in wanted:
@@ -315,7 +367,7 @@
         crossed_in(0, f).wait_recv()
         for p in range(2):
             for l in range(2):
-                out_buf[p, f, l] = state[p, f, l, pl.ds(HALO, ROWS), :] - (own[3, f, p, l] + crossed[0, f, p, l])
+                out_buf[p, f, l] = state[p, f, l, pl.ds(BASE, ROWS), :] - (own[3, f, p, l] + crossed[0, f, p, l])
         return carry
 
     lax.fori_loop(0, 3, m1, 0)
@@ -330,14 +382,9 @@
     passed.wait_recv()
     for f in range(3):
         for l in range(2):
-            before_first = jnp.where(tm == 0, state[2, f, l, pl.ds(HALO, ROWS), :], prev[f, l])
-            res_buf[0, f, l] = powers[0, 0, f, l, pl.ds(HALO, ROWS), :] - before_first
-            res_buf[1, f, l] = powers[0, 1, f, l, pl.ds(HALO, ROWS), :]
-    stores = [pltpu.make_async_copy(res_buf.at[:, :, l], res_out.at[:, :, :, pl.ds(128 * l, 128)], store_sem.at[l])
-              for l in range(2)]
-    for store in stores:
-        store.start()
-
+            before_first = jnp.where(tm == 0, state[2, f, l, pl.ds(BASE, ROWS), :], prev[f, l])
+            res_buf[0, f, l] = powers[0, 0, f, l, pl.ds(BASE, ROWS), :] - before_first
+            res_buf[1, f, l] = powers[0, 1, f, l, pl.ds(BASE, ROWS), :]
     def finish(f, carry):
         for side in range(2):
             near_copy(side, f).wait_recv()
@@ -348,11 +395,6 @@
         return carry
 
     lax.fori_loop(0, 3, finish, 0)
-    ends = [pltpu.make_async_copy(out_buf.at[:, :, l], upd_out.at[:, :, :, pl.ds(128 * l, 128)], store_sem.at[2 + l])
-            for l in range(2)]
-    for end in ends:
-        end.start()
-
     for copy in halo:
         copy.wait_send()
 
@@ -373,35 +415,48 @@
         return carry
 
     lax.fori_loop(0, 3, drain, 0)
-    for store in stores + ends:
-        store.wait()
+
+
+def put_out(upd_in, res_in, upd_out, res_out, sem):
+    copies = []
+    for l in range(2):
+        columns = pl.ds(128 * l, 128)
+        copies.append(pltpu.make_async_copy(upd_in.at[:, :, l], upd_out.at[:, :, :, columns], sem.at[l]))
+        copies.append(pltpu.make_async_copy(res_in.at[:, :, l], res_out.at[:, :, :, columns], sem.at[2 + l]))
+    for copy in copies:
+        copy.start()
+    for copy in copies:
+        copy.wait()
 
 
 def shards(trajectory, initial):
     whole = jax.ShapeDtypeStruct(trajectory.shape, F32)
     anywhere = pl.BlockSpec(memory_space=pl.ANY)
+    slow = pl.BlockSpec(memory_space=pltpu.HBM)
+    fast = pl.BlockSpec(memory_space=pltpu.VMEM)
     dma = pltpu.SemaphoreType.DMA
-    return pl.pallas_call(
+    tiles = pltpu.VMEM((2, 3, 2, ROWS, 128), F32)
+    updated, residual = pl.pallas_call(
         kernel,
-        out_shape=(whole, whole),
-        in_specs=[anywhere, anywhere],
-        out_specs=(anywhere, anywhere),
+        out_shape=(tiles, tiles),
+        in_specs=[slow, slow],
+        out_specs=(fast, fast),
         scratch_shapes=[
-            pltpu.VMEM((3, 3, 3, TALL, 128), F32),
-            pltpu.VMEM((CHEB + 1, 3, 3, 3, TALL, 128), F32),
+            pltpu.VMEM((3, 3, 3, DEEP, 128), F32),
+            pltpu.VMEM((CHEB + 1, 3, 3, 3, DEEP, 128), F32),
+            pltpu.VMEM((TALL, 128), F32),
             pltpu.VMEM((3, 2, ROWS, 128), F32),
             pltpu.VMEM((ROWS, 128), F32),
             pltpu.VMEM((ROWS, 128), F32),
             pltpu.VMEM((TALL, 128), F32),
             pltpu.VMEM((TALL, 128), F32),
-            pltpu.VMEM((2, 3, 2, ROWS, 128), F32),
             pltpu.VMEM((4, 3, 2, 2, ROWS, 128), F32),
             pltpu.VMEM((4, 3, 2, 2, ROWS, 128), F32),
             pltpu.VMEM((4, 3, 2, 2, ROWS, 128), F32),
             pltpu.VMEM((2, 3, 2, ROWS, 128), F32),
             pltpu.VMEM((2, 3, 2, ROWS, 128), F32),
             pltpu.VMEM((2, 3, 2, ROWS, 128), F32),
-            pltpu.VMEM((2, 3, 2, ROWS, 128), F32),
+            pltpu.SemaphoreType.REGULAR((12,)),
             dma((4,)),
             dma((11,)),
             dma((11,)),
@@ -409,11 +464,19 @@
             dma((4, 3)),
             dma((3, 2, 3)),
             dma((3, 2, 3)),
-            dma((4,)),
         ],
         compiler_params=pltpu.CompilerParams(collective_id=0, has_side_effects=True),
         name="paradiag",
     )(trajectory, initial)
+    return pl.pallas_call(
+        put_out,
+        out_shape=(whole, whole),
+        in_specs=[anywhere, anywhere],
+        out_specs=(anywhere, anywhere),
+        scratch_shapes=[dma((4,))],
+        compiler_params=pltpu.CompilerParams(vmem_limit_bytes=4 << 20),
+        name="put_out",
+    )(updated, residual)
 
 
 def solution(mesh):

time: 31.7 us -> 29.5 us (0.931)
  local copies, waits for them, and re-layouts: 2.34 us -> 0 us
    unnamed x4 -> x0, local copies, waits for them, and re-layouts: 2.34 us -> none
    pallas_call x1 -> x2, Pallas kernels: 28.5 us -> 28.7 us  [the longest x1 27.9 us: shards(): pl.pallas_call(kernel, out_shape=(tiles, tiles), in_specs=[slow, slow], o...]
where the time goes in v2:
time: 29.5 us; the launch traced here: 29.4 us
  Pallas kernels  28.7 us (97%)
  between operations  0.64 us (2%)
    pallas_call x1, Pallas kernels, shards(): pl.pallas_call(kernel, out_shape=(tiles, tiles), in_specs=[slow, slow], o...  27.9 us
    pallas_call x1, Pallas kernels, shards(): pl.pallas_call(put_out, out_shape=(whole, whole), in_specs=[anywhere, any...  0.78 us

profile of v2, /device:TPU:1, one launch (start us, length us, event | category | flops | bytes accessed | tf_op | source)
XLA Modules:
  0.0 29.4 jit_solution(5872574013291293350)
XLA Ops:
  0.6 27.9 %paradiag.1 = (f32[2,3,2,32,128]{4,3,2,1,0:T(8,128)S(1)}, f32[2,3,2,32,128]{4,3,2,1,0:T(8,128)S(1)}) custom-call(f32[2,3,32,256]{3,2,1,0:T(8,128)} %traj.1, f32[3,32,256]{2,1,0:T(8,128)} %init.1), custom_call_target="tpu_custom_call" | custom-call | tf_op jit(solution)/shard_map/paradiag/pallas_call | solution.py:439
  28.6 0.8 %put_out.1 = (f32[2,3,32,256]{3,2,1,0:T(8,128)}, f32[2,3,32,256]{3,2,1,0:T(8,128)}) custom-call(f32[2,3,2,32,128]{4,3,2,1,0:T(8,128)S(1)} %get-tuple-element.4.upd_in, f32[2,3,2,32,128]{4,3,2,1,0:T(8,128)S(1)} %get-tuple-element.5.res_in), custom_call_target="tpu_custom_call" | custom-call | tf_op jit(solution)/shard_map/put_out/pallas_call | solution.py:471

commit v3 on v2

v3 whole, which is shorter than its diff:
```python
import math

import jax
import jax.numpy as jnp
import numpy as np
from jax import lax
from jax.experimental import pallas as pl
from jax.experimental.pallas import tpu as pltpu
from jax.sharding import PartitionSpec as P

MESH = pl.DeviceIdType.MESH
F32 = jnp.float32

CHEB = 6
STEPS = 16
courant = 1.5
coriolis_mean = 0.3
coriolis_slope = 0.4
circulant = 0.1
spectrum_edge = 5.0

HALO = 8
ROWS = 32
TALL = ROWS + 2 * HALO
EDGE = 8
BASE = EDGE + HALO
DEEP = TALL + 2 * EDGE
WRAPS = 1.0 / circulant
OPPOSITE = (1, 0, 5, 6, 7, 2, 3, 4, 8, 8, 8, 8)
(LOAD, HALO_S, HALO_R, OPEN_S, OPEN_R, PASS_S, PASS_R, CROSS_S, RING_S, CROSS_FAR, CROSS_NEAR, CROSS_OWN, RING_FAR,
 RING_END, N_SEM) = (0, 1, 2, 3, 4, 5, 6, 7, 8, 9, 12, 15, 16, 19, 22)


def power_table():
    beta = circulant ** (1.0 / STEPS)
    solved = np.zeros((STEPS, CHEB + 1), complex)
    for k in range(STEPS):
        theta = 2.0 * np.pi * k / STEPS
        shift = 1.0 - beta * np.cos(theta) + 1j * beta * np.sin(theta)
        edge = 1j * spectrum_edge
        sigma = shift / edge
        rho_old = 1.0 / sigma
        one = np.zeros(CHEB + 2, complex)
        one[0] = 1.0
        update = one / shift
        total = update.copy()
        for _ in range(CHEB):
            misfit = one - (shift * total + np.roll(total, 1))
            rho_new = 1.0 / (2.0 * sigma - rho_old)
            update = rho_new * rho_old * update + 2.0 * rho_new / edge * misfit
            total = total + update
            rho_old = rho_new
        solved[k] = total[: CHEB + 1]
    turns = np.exp(2j * np.pi / STEPS * np.outer(np.arange(STEPS), np.arange(STEPS)))
    table = (turns @ solved).real / STEPS
    return table * courant ** np.arange(CHEB + 1)


TABLE = power_table()


def weight(delta, p, q, m):
    difference = 2 * delta + p - q
    return float(circulant ** (-difference / STEPS) * TABLE[difference % STEPS, m])


def kernel(
    traj, init, out_buf, res_buf,
    state, powers, rotation, prev, strip_l, strip_r, edge_l, edge_r,
    cross, crossed, own, relay, near_a, near_b,
    ready, sem,
):
    tm, gx, gy = lax.axis_index("tm"), lax.axis_index("gx"), lax.axis_index("gy")
    n_tm, n_gx, n_gy = lax.axis_size("tm"), lax.axis_size("gx"), lax.axis_size("gy")
    core = lax.rem(tm, 2)
    east, west = lax.rem(gx + 1, n_gx), lax.rem(gx + n_gx - 1, n_gx)
    north, south = lax.rem(gy + 1, n_gy), lax.rem(gy + n_gy - 1, n_gy)
    after, before = lax.rem(tm + 1, n_tm), lax.rem(tm + n_tm - 1, n_tm)
    chip_up, chip_down = lax.rem(tm + 2, n_tm), lax.rem(tm + n_tm - 2, n_tm)
    partner = tm + 1 - 2 * core
    last = tm == n_tm - 1

    loads = []
    for lane in range(2):
        columns = pl.ds(128 * lane, 128)
        loads.append(pltpu.make_async_copy(
            traj.at[:, :, :, columns], state.at[pl.ds(0, 2), :, lane, pl.ds(BASE, ROWS), :], sem.at[LOAD]))
        loads.append(pltpu.make_async_copy(
            init.at[:, :, columns], state.at[2, :, lane, pl.ds(BASE, ROWS), :], sem.at[LOAD]))
    for load in loads:
        load.start()
    loaded = state.at[:, :, pl.ds(0, 2), pl.ds(BASE, ROWS), :]

    def arrival(t, x, y):
        by_z = jnp.minimum(2 * y + 2 * jnp.minimum(y, 1), 11)
        return (t // 2 + x + by_z + 1 - t % 2) * 256 + t * 32 + x * 8 + y

    across = jnp.where(core == 1, after, before)
    peers = [(tm, east, gy), (tm, west, gy), (tm, gx, north), (tm, east, north), (tm, west, north),
             (tm, gx, south), (tm, west, south), (tm, east, south),
             (partner, gx, gy), (chip_up, gx, gy), (chip_down, gx, gy), (across, gx, gy)]
    mine = arrival(tm, gx, gy)
    earlier = [(arrival(*peer) < mine).astype(jnp.int32) for peer in peers]

    barrier = pltpu.get_barrier_semaphore()
    for peer, sooner in zip(peers, earlier, strict=True):
        @pl.when(sooner == 0)
        def _(peer=peer):
            pl.semaphore_signal(barrier, inc=1, device_id=peer, device_id_type=MESH)

    sooner_count = sum(earlier)

    @pl.when(sooner_count > 0)
    def _():
        pl.semaphore_wait(barrier, sooner_count)

    for i, (peer, sooner) in enumerate(zip(peers, earlier, strict=True)):
        @pl.when(sooner == 1)
        def _(i=i, peer=peer):
            pl.semaphore_signal(ready.at[OPPOSITE[i]], inc=1, device_id=peer, device_id_type=MESH)

    pltpu.make_async_copy(loaded, loaded, sem.at[LOAD]).wait()

    lane_id = lax.broadcasted_iota(jnp.int32, (TALL, 128), 1)
    packed_l = jnp.zeros((ROWS, 128), F32)
    packed_r = jnp.zeros((ROWS, 128), F32)
    for s in range(3):
        for f in range(3):
            spot = 8 * (3 * s + f)
            here = (lane_id[:ROWS] >= spot) & (lane_id[:ROWS] < spot + 8)
            left = state[s, f, 0, pl.ds(BASE, ROWS), :]
            right = state[s, f, 1, pl.ds(BASE, ROWS), :]
            packed_l = jnp.where(here, pltpu.roll(left, spot, 1) if spot else left, packed_l)
            packed_r = jnp.where(here, pltpu.roll(right, spot + 8, 1), packed_r)
    strip_l[...] = packed_l
    strip_r[...] = packed_r

    def remote(src, dst, send, recv, peer):
        return pltpu.make_async_remote_copy(
            src_ref=src, dst_ref=dst, send_sem=send, recv_sem=recv, device_id=peer, device_id_type=MESH)

    top, bottom, low, high = pl.ds(0, HALO), pl.ds(ROWS - HALO, HALO), pl.ds(BASE, HALO), pl.ds(EDGE + ROWS, HALO)
    first, final = pl.ds(0, HALO), pl.ds(HALO + ROWS, HALO)
    under, over = pl.ds(EDGE, HALO), pl.ds(BASE + ROWS, HALO)
    both, cols = pl.ds(0, 2), pl.ds(0, 2)
    middle = pl.ds(HALO, ROWS)
    sides = [
        (strip_r, edge_l.at[middle]),
        (strip_l, edge_r.at[middle]),
        (state.at[both, :, cols, high, :], state.at[both, :, cols, under, :]),
        (strip_r.at[bottom], edge_l.at[first]),
        (strip_l.at[bottom], edge_r.at[first]),
        (state.at[both, :, cols, low, :], state.at[both, :, cols, over, :]),
        (strip_l.at[top], edge_r.at[final]),
        (strip_r.at[top], edge_l.at[final]),
    ]
    halo = [remote(src, dst, sem.at[HALO_S], sem.at[HALO_R], peers[i]) for i, (src, dst) in enumerate(sides)]
    opening = [
        remote(state.at[2, :, cols, high, :], state.at[2, :, cols, under, :], sem.at[OPEN_S], sem.at[OPEN_R],
               (tm, gx, north)),
        remote(state.at[2, :, cols, low, :], state.at[2, :, cols, over, :], sem.at[OPEN_S], sem.at[OPEN_R],
               (tm, gx, south)),
    ]
    passed = remote(state.at[1, :, cols, pl.ds(BASE, ROWS), :], prev, sem.at[PASS_S], sem.at[PASS_R], (after, gx, gy))
    for i in range(8):
        @pl.when(earlier[i] == 1)
        def _(i=i):
            halo[i].start()
    for i in range(8):
        @pl.when(earlier[i] == 0)
        def _(i=i):
            pl.semaphore_wait(ready.at[i], 1)
            halo[i].start()

    @pl.when(last)
    def _():
        for copy in opening:
            copy.start()

    later_count = 4 - sum(earlier[8:])

    @pl.when(later_count > 0)
    def _():
        pl.semaphore_wait(ready.at[8], later_count)

    passed.start()

    def await_bytes(ref, i):
        pltpu.make_async_copy(ref, ref, sem.at[i]).wait()

    halo_bytes, opening_bytes = state.at[:, :, 0, pl.ds(0, ROWS), :], state.at[2, :, cols, pl.ds(0, 2 * HALO), :]
    await_bytes(halo_bytes, HALO_R)

    @pl.when(last)
    def _():
        await_bytes(opening_bytes, OPEN_R)

    tall = pl.ds(EDGE, TALL)
    for s in range(3):
        for f in range(3):
            spot = 8 * (3 * s + f)
            right = pltpu.roll(edge_r[...], (128 - spot) % 128, 1) if spot else edge_r[...]
            left = pltpu.roll(edge_l[...], 120 - spot, 1)
            state[s, f, 2, tall, :] = jnp.where(lane_id < 64, right, left)

    row = (gy * ROWS - HALO + n_gy * ROWS + lax.broadcasted_iota(jnp.int32, (TALL, 128), 0)) % (n_gy * ROWS)
    latitude = coriolis_mean + coriolis_slope * ((row.astype(F32) + 0.5) / (n_gy * ROWS) - 0.5)
    rotation[...] = latitude * (1.0 / courant)


    def dx(tiles):
        ahead = [pltpu.roll(t, 127, 1) for t in tiles]
        behind = [pltpu.roll(t, 1, 1) for t in tiles]
        lane = lane_id[: tiles[0].shape[0]]
        return [jnp.where(lane == 127, ahead[(l + 1) % 3], ahead[l]) - jnp.where(lane == 0, behind[(l + 2) % 3], behind[l])
                for l in range(3)]

    above, below = pl.ds(EDGE + 1, TALL), pl.ds(EDGE - 1, TALL)

    def start_fields(s, carry):
        h = [state[s, 0, l, tall, :] for l in range(3)]
        u = [state[s, 1, l, tall, :] for l in range(3)]
        v = [state[s, 2, l, tall, :] for l in range(3)]
        turn = rotation[...]
        flux = dx([u[l] + h[l] * u[l] for l in range(3)])
        slope_h, slope_u, slope_v = dx(h), dx(u), dx(v)
        for l in range(3):
            (ha, hb), (ua, ub), (va, vb) = [(state[s, f, l, above, :], state[s, f, l, below, :]) for f in range(3)]
            powers[0, s, 0, l, tall, :] = h[l] + courant * (flux[l] + ((va + ha * va) - (vb + hb * vb)))
            powers[0, s, 1, l, tall, :] = u[l] + courant * (
                slope_h[l] - turn * v[l] + (u[l] * slope_u[l] + v[l] * (ua - ub)))
            powers[0, s, 2, l, tall, :] = v[l] + courant * (
                (ha - hb) + turn * u[l] + (u[l] * slope_v[l] + v[l] * (va - vb)))
        return carry

    lax.fori_loop(0, 2, start_fields, 0)

    slot = jnp.where(last, 2, 1)
    factor = jnp.where(last, -WRAPS, -1.0).astype(F32)
    for f in range(3):
        for l in range(3):
            powers[0, 2, f, l, tall, :] = factor * state[slot, f, l, tall, :]
            powers[0, 1, f, l, tall, :] = powers[0, 1, f, l, tall, :] - state[0, f, l, tall, :]

    def next_power(m, carry):
        for q in range(3):
            h = [powers[m, q, 0, l, tall, :] for l in range(3)]
            u = [powers[m, q, 1, l, tall, :] for l in range(3)]
            slope_h, slope_u = dx(h), dx(u)
            turn = rotation[...]
            for l in range(3):
                ha, hb = powers[m, q, 0, l, above, :], powers[m, q, 0, l, below, :]
                va, vb = powers[m, q, 2, l, above, :], powers[m, q, 2, l, below, :]
                v = powers[m, q, 2, l, tall, :]
                powers[m + 1, q, 0, l, tall, :] = slope_u[l] + (va - vb)
                powers[m + 1, q, 1, l, tall, :] = slope_h[l] - turn * v
                powers[m + 1, q, 2, l, tall, :] = (ha - hb) + turn * u[l]
        return carry

    lax.fori_loop(0, CHEB - 1, next_power, 0)

    block, block_up, block_down = pl.ds(BASE, ROWS), pl.ds(BASE + 1, ROWS), pl.ds(BASE - 1, ROWS)
    m = CHEB - 1
    for q in range(3):
        h = [powers[m, q, 0, l, block, :] for l in range(3)]
        u = [powers[m, q, 1, l, block, :] for l in range(3)]
        slope_h, slope_u = dx(h), dx(u)
        turn = rotation[pl.ds(HALO, ROWS), :]
        for l in range(2):
            ha, hb = powers[m, q, 0, l, block_up, :], powers[m, q, 0, l, block_down, :]
            va, vb = powers[m, q, 2, l, block_up, :], powers[m, q, 2, l, block_down, :]
            v = powers[m, q, 2, l, block, :]
            powers[m + 1, q, 0, l, block, :] = slope_u[l] + (va - vb)
            powers[m + 1, q, 1, l, block, :] = slope_h[l] - turn * v
            powers[m + 1, q, 2, l, block, :] = (ha - hb) + turn * u[l]

    def mix(f, wanted):
        def body(l, carry):
            totals = [None] * len(wanted)
            for q in range(3):
                for m in range(CHEB + 1):
                    value = powers[m, q, f, l, block, :]
                    for i, (delta, p, _, _) in enumerate(wanted):
                        term = weight(delta, p, q, m) * value
                        totals[i] = term if totals[i] is None else totals[i] + term
            for (delta, p, ref, index), total in zip(wanted, totals, strict=True):
                if delta:
                    total = total * jnp.where(tm + delta >= n_tm, circulant, 1.0).astype(F32)
                ref[(*index, l)] = total
            return carry
        lax.fori_loop(0, 2, body, 0)

    def both_steps(delta, ref, *index):
        return [(delta, p, ref, (*index, p)) for p in range(2)]

    def send_across(place, f):
        i = {0: CROSS_OWN, 1: CROSS_NEAR + f, 2: CROSS_FAR + f, 3: CROSS_NEAR + f}[place]
        remote(cross.at[place, f], crossed.at[place, f], sem.at[CROSS_S], sem.at[i], (partner, gx, gy)).start()

    def odd_delta(seat, place):
        return (2 * place + 1 - 2 * seat) % 8

    def for_partner(f, places):
        for seat in range(2):
            @pl.when(core == seat)
            def _(seat=seat):
                mix(f, [w for place in places for w in both_steps(odd_delta(seat, place), cross, place, f)])
        for place in places:
            send_across(place, f)

    up, down = (chip_up, gx, gy), (chip_down, gx, gy)

    def send_ring(i, side, src, dst):
        remote(src, dst, sem.at[RING_S], sem.at[i], down if side else up).start()

    def far_odd(f, carry):
        for_partner(f, (2,))
        return carry

    def far_even(f, carry):
        mix(f, both_steps(4, own, 0, f))
        return carry

    def far_out(f, carry):
        for_partner(f, (1, 3))
        await_bytes(crossed.at[2, f], CROSS_FAR + f)
        own[0, f] = own[0, f] + crossed[2, f]
        for side in range(2):
            send_ring(RING_FAR + f, side, own.at[0, f, side], relay.at[side, f])
        return carry

    def near_out(f, carry):
        mix(f, both_steps(2, own, 1, f) + both_steps(6, own, 2, f))
        await_bytes(crossed.at[pl.ds(0, 2), f], CROSS_NEAR + f)
        own[1, f] = own[1, f] + crossed[1, f]
        own[2, f] = own[2, f] + crossed[3, f]
        for side in range(2):
            send_ring(RING_END + f, side, own.at[1 + side, f, 1 - side], near_a.at[side, f])
        return carry

    def here_odd(f, carry):
        for_partner(f, (0,))
        return carry

    def here_even(f, carry):
        mix(f, both_steps(0, own, 3, f))
        return carry

    def relay_out(f, carry):
        await_bytes(relay.at[:, f], RING_FAR + f)
        for side in range(2):
            own[1 + side, f, side] = own[1 + side, f, side] + relay[side, f]
            send_ring(RING_END + f, side, own.at[1 + side, f, side], near_b.at[side, f])
        return carry

    lax.fori_loop(0, 3, far_odd, 0)
    lax.fori_loop(0, 3, far_even, 0)
    lax.fori_loop(0, 3, far_out, 0)
    lax.fori_loop(0, 3, near_out, 0)
    lax.fori_loop(0, 3, here_odd, 0)
    lax.fori_loop(0, 3, here_even, 0)
    lax.fori_loop(0, 3, relay_out, 0)

    await_bytes(prev, PASS_R)
    await_bytes(crossed.at[0], CROSS_OWN)
    for f in range(3):
        for l in range(2):
            before_first = jnp.where(tm == 0, state[2, f, l, block, :], prev[f, l])
            res_buf[0, f, l] = powers[0, 0, f, l, block, :] - before_first
            res_buf[1, f, l] = powers[0, 1, f, l, block, :]
            for p in range(2):
                out_buf[p, f, l] = state[p, f, l, block, :] - (own[3, f, p, l] + crossed[0, f, p, l])

    await_bytes(halo_bytes, HALO_S)

    @pl.when(last)
    def _():
        await_bytes(opening_bytes, OPEN_S)

    await_bytes(prev, PASS_S)
    await_bytes(cross, CROSS_S)

    def finish(f, carry):
        await_bytes(own.at[pl.ds(0, 2), f], RING_END + f)
        for l in range(2):
            out_buf[0, f, l] = out_buf[0, f, l] - (near_b[0, f, l] + near_a[1, f, l])
            out_buf[1, f, l] = out_buf[1, f, l] - (near_a[0, f, l] + near_b[1, f, l])
        return carry

    lax.fori_loop(0, 3, finish, 0)
    await_bytes(own.at[pl.ds(0, 3)], RING_S)


def put_out(upd_in, res_in, upd_out, res_out, sem):
    copies = []
    for l in range(2):
        columns = pl.ds(128 * l, 128)
        copies.append(pltpu.make_async_copy(upd_in.at[:, :, l], upd_out.at[:, :, :, columns], sem.at[l]))
        copies.append(pltpu.make_async_copy(res_in.at[:, :, l], res_out.at[:, :, :, columns], sem.at[2 + l]))
    for copy in copies:
        copy.start()
    for copy in copies:
        copy.wait()


def shards(trajectory, initial):
    whole = jax.ShapeDtypeStruct(trajectory.shape, F32)
    anywhere = pl.BlockSpec(memory_space=pl.ANY)
    slow = pl.BlockSpec(memory_space=pltpu.HBM)
    fast = pl.BlockSpec(memory_space=pltpu.VMEM)
    dma = pltpu.SemaphoreType.DMA
    tiles = pltpu.VMEM((2, 3, 2, ROWS, 128), F32)
    updated, residual = pl.pallas_call(
        kernel,
        out_shape=(tiles, tiles),
        in_specs=[slow, slow],
        out_specs=(fast, fast),
        scratch_shapes=[
            pltpu.VMEM((3, 3, 3, DEEP, 128), F32),
            pltpu.VMEM((CHEB + 1, 3, 3, 3, DEEP, 128), F32),
            pltpu.VMEM((TALL, 128), F32),
            pltpu.VMEM((3, 2, ROWS, 128), F32),
            pltpu.VMEM((ROWS, 128), F32),
            pltpu.VMEM((ROWS, 128), F32),
            pltpu.VMEM((TALL, 128), F32),
            pltpu.VMEM((TALL, 128), F32),
            pltpu.VMEM((4, 3, 2, 2, ROWS, 128), F32),
            pltpu.VMEM((4, 3, 2, 2, ROWS, 128), F32),
            pltpu.VMEM((4, 3, 2, 2, ROWS, 128), F32),
            pltpu.VMEM((2, 3, 2, ROWS, 128), F32),
            pltpu.VMEM((2, 3, 2, ROWS, 128), F32),
            pltpu.VMEM((2, 3, 2, ROWS, 128), F32),
            pltpu.SemaphoreType.REGULAR((9,)),
            dma((N_SEM,)),
        ],
        compiler_params=pltpu.CompilerParams(collective_id=0, has_side_effects=True),
        name="paradiag",
    )(trajectory, initial)
    return pl.pallas_call(
        put_out,
        out_shape=(whole, whole),
        in_specs=[anywhere, anywhere],
        out_specs=(anywhere, anywhere),
        scratch_shapes=[dma((4,))],
        compiler_params=pltpu.CompilerParams(vmem_limit_bytes=4 << 20),
        name="put_out",
    )(updated, residual)


def solution(mesh):
    in_specs = (P("tm", None, "gy", "gx"), P(None, "gy", "gx"))
    out_specs = (P("tm", None, "gy", "gx"), P("tm", None, "gy", "gx"))
    return jax.shard_map(shards, mesh=mesh, in_specs=in_specs, out_specs=out_specs, check_vma=False)
```

time: 29.5 us -> 28.4 us (0.963)
  Pallas kernels: 28.7 us -> 27.6 us
    pallas_call x1, Pallas kernels: 27.9 us -> 26.8 us  [shards(): pl.pallas_call(kernel, out_shape=(tiles, tiles), in_specs=[slow, slow], o...]
where the time goes in v3:
time: 28.4 us; the launch traced here: 28.3 us
  Pallas kernels  27.6 us (97%)
  between operations  0.64 us (2%)
    pallas_call x1, Pallas kernels, shards(): pl.pallas_call(kernel, out_shape=(tiles, tiles), in_specs=[slow, slow], o...  26.8 us
    pallas_call x1, Pallas kernels, shards(): pl.pallas_call(put_out, out_shape=(whole, whole), in_specs=[anywhere, any...  0.78 us

profile of v3, /device:TPU:1, one launch (start us, length us, event | category | flops | bytes accessed | tf_op | source)
XLA Modules:
  0.0 28.3 jit_solution(14407890095310847027)
XLA Ops:
  0.6 26.8 %paradiag.1 = (f32[2,3,2,32,128]{4,3,2,1,0:T(8,128)S(1)}, f32[2,3,2,32,128]{4,3,2,1,0:T(8,128)S(1)}) custom-call(f32[2,3,32,256]{3,2,1,0:T(8,128)} %traj.1, f32[3,32,256]{2,1,0:T(8,128)} %init.1), custom_call_target="tpu_custom_call" | custom-call | tf_op jit(solution)/shard_map/paradiag/pallas_call | solution.py:413
  27.5 0.8 %put_out.1 = (f32[2,3,32,256]{3,2,1,0:T(8,128)}, f32[2,3,32,256]{3,2,1,0:T(8,128)}) custom-call(f32[2,3,2,32,128]{4,3,2,1,0:T(8,128)S(1)} %get-tuple-element.4.upd_in, f32[2,3,2,32,128]{4,3,2,1,0:T(8,128)S(1)} %get-tuple-element.5.res_in), custom_call_target="tpu_custom_call" | custom-call | tf_op jit(solution)/shard_map/put_out/pallas_call | solution.py:439

commit v4 on v3

--- a/solution.py
+++ b/solution.py
@@ -27,8 +27,9 @@
 DEEP = TALL + 2 * EDGE
 WRAPS = 1.0 / circulant
 OPPOSITE = (1, 0, 5, 6, 7, 2, 3, 4, 8, 8, 8, 8)
-(LOAD, HALO_S, HALO_R, OPEN_S, OPEN_R, PASS_S, PASS_R, CROSS_S, RING_S, CROSS_FAR, CROSS_NEAR, CROSS_OWN, RING_FAR,
- RING_END, N_SEM) = (0, 1, 2, 3, 4, 5, 6, 7, 8, 9, 12, 15, 16, 19, 22)
+MOST, REST = 24, 8
+(LOAD, HALO_S, HALO_Y, HALO_SIDE, OPEN_S, OPEN_SIDE, PASS_S, PASS_R, CROSS_S, RING_S, CROSS_FAR, CROSS_NEAR, CROSS_OWN, RING_FAR,
+ RING_END, N_SEM) = (0, 1, 2, 3, 5, 6, 8, 9, 10, 11, 12, 16, 20, 21, 25, 29)
 
 
 def power_table():
@@ -67,7 +68,7 @@
 def kernel(
     traj, init, out_buf, res_buf,
     state, powers, rotation, prev, strip_l, strip_r, edge_l, edge_r,
-    cross, crossed, own, relay, near_a, near_b,
+    side_in, cross, crossed, own, relay, near_a, near_b,
     ready, sem,
 ):
     tm, gx, gy = lax.axis_index("tm"), lax.axis_index("gx"), lax.axis_index("gy")
@@ -141,24 +142,24 @@
 
     top, bottom, low, high = pl.ds(0, HALO), pl.ds(ROWS - HALO, HALO), pl.ds(BASE, HALO), pl.ds(EDGE + ROWS, HALO)
     first, final = pl.ds(0, HALO), pl.ds(HALO + ROWS, HALO)
-    under, over = pl.ds(EDGE, HALO), pl.ds(BASE + ROWS, HALO)
     both, cols = pl.ds(0, 2), pl.ds(0, 2)
     middle = pl.ds(HALO, ROWS)
     sides = [
         (strip_r, edge_l.at[middle]),
         (strip_l, edge_r.at[middle]),
-        (state.at[both, :, cols, high, :], state.at[both, :, cols, under, :]),
+        (state.at[both, :, cols, high, :], side_in.at[0, both]),
         (strip_r.at[bottom], edge_l.at[first]),
         (strip_l.at[bottom], edge_r.at[first]),
-        (state.at[both, :, cols, low, :], state.at[both, :, cols, over, :]),
+        (state.at[both, :, cols, low, :], side_in.at[1, both]),
         (strip_l.at[top], edge_r.at[final]),
         (strip_r.at[top], edge_l.at[final]),
     ]
-    halo = [remote(src, dst, sem.at[HALO_S], sem.at[HALO_R], peers[i]) for i, (src, dst) in enumerate(sides)]
+    seats = (HALO_Y, HALO_Y, HALO_SIDE, HALO_SIDE, HALO_SIDE, HALO_SIDE + 1, HALO_SIDE + 1, HALO_SIDE + 1)
+    halo = [remote(src, dst, sem.at[HALO_S], sem.at[seats[i]], peers[i]) for i, (src, dst) in enumerate(sides)]
     opening = [
-        remote(state.at[2, :, cols, high, :], state.at[2, :, cols, under, :], sem.at[OPEN_S], sem.at[OPEN_R],
+        remote(state.at[2, :, cols, high, :], side_in.at[0, 2], sem.at[OPEN_S], sem.at[OPEN_SIDE],
                (tm, gx, north)),
-        remote(state.at[2, :, cols, low, :], state.at[2, :, cols, over, :], sem.at[OPEN_S], sem.at[OPEN_R],
+        remote(state.at[2, :, cols, low, :], side_in.at[1, 2], sem.at[OPEN_S], sem.at[OPEN_SIDE + 1],
                (tm, gx, south)),
     ]
     passed = remote(state.at[1, :, cols, pl.ds(BASE, ROWS), :], prev, sem.at[PASS_S], sem.at[PASS_R], (after, gx, gy))
@@ -188,25 +189,35 @@
     def await_bytes(ref, i):
         pltpu.make_async_copy(ref, ref, sem.at[i]).wait()
 
-    halo_bytes, opening_bytes = state.at[:, :, 0, pl.ds(0, ROWS), :], state.at[2, :, cols, pl.ds(0, 2 * HALO), :]
-    await_bytes(halo_bytes, HALO_R)
-
-    @pl.when(last)
-    def _():
-        await_bytes(opening_bytes, OPEN_R)
-
-    tall = pl.ds(EDGE, TALL)
-    for s in range(3):
-        for f in range(3):
-            spot = 8 * (3 * s + f)
-            right = pltpu.roll(edge_r[...], (128 - spot) % 128, 1) if spot else edge_r[...]
-            left = pltpu.roll(edge_l[...], 120 - spot, 1)
-            state[s, f, 2, tall, :] = jnp.where(lane_id < 64, right, left)
+    halo_bytes, y_bytes = state.at[:, :, 0, pl.ds(0, ROWS), :], relay.at[0, 0]
+    side_bytes = powers.at[:, 0, 0, 0, pl.ds(0, 2 * HALO), :]
+    opening_bytes, opening_side = state.at[2, :, cols, pl.ds(0, 2 * HALO), :], state.at[2, :, cols, pl.ds(0, HALO), :]
+
+    late = jnp.minimum(gy, 1) * jnp.minimum(n_gy - 1 - gy, 1)
+
+    def await_side(side):
+        await_bytes(side_bytes, HALO_SIDE + side)
+
+        @pl.when(last)
+        def _():
+            await_bytes(opening_side, OPEN_SIDE + side)
+
+        state[:, :, cols, pl.ds(pl.multiple_of(EDGE + (HALO + ROWS) * side, 8), HALO), :] = side_in[side]
 
     row = (gy * ROWS - HALO + n_gy * ROWS + lax.broadcasted_iota(jnp.int32, (TALL, 128), 0)) % (n_gy * ROWS)
     latitude = coriolis_mean + coriolis_slope * ((row.astype(F32) + 0.5) / (n_gy * ROWS) - 0.5)
     rotation[...] = latitude * (1.0 / courant)
 
+    def spread_edges(start, count):
+        here = pl.ds(pl.multiple_of(start, 8), count)
+        there = pl.ds(pl.multiple_of(EDGE + start, 8), count)
+        for s in range(3):
+            for f in range(3):
+                spot = 8 * (3 * s + f)
+                packed = edge_r[here, :]
+                right = pltpu.roll(packed, (128 - spot) % 128, 1) if spot else packed
+                left = pltpu.roll(edge_l[here, :], 120 - spot, 1)
+                state[s, f, 2, there, :] = jnp.where(lane_id[:count] < 64, right, left)
 
     def dx(tiles):
         ahead = [pltpu.roll(t, 127, 1) for t in tiles]
@@ -215,151 +226,198 @@
         return [jnp.where(lane == 127, ahead[(l + 1) % 3], ahead[l]) - jnp.where(lane == 0, behind[(l + 2) % 3], behind[l])
                 for l in range(3)]
 
-    above, below = pl.ds(EDGE + 1, TALL), pl.ds(EDGE - 1, TALL)
-
-    def start_fields(s, carry):
-        h = [state[s, 0, l, tall, :] for l in range(3)]
-        u = [state[s, 1, l, tall, :] for l in range(3)]
-        v = [state[s, 2, l, tall, :] for l in range(3)]
-        turn = rotation[...]
-        flux = dx([u[l] + h[l] * u[l] for l in range(3)])
-        slope_h, slope_u, slope_v = dx(h), dx(u), dx(v)
-        for l in range(3):
-            (ha, hb), (ua, ub), (va, vb) = [(state[s, f, l, above, :], state[s, f, l, below, :]) for f in range(3)]
-            powers[0, s, 0, l, tall, :] = h[l] + courant * (flux[l] + ((va + ha * va) - (vb + hb * vb)))
-            powers[0, s, 1, l, tall, :] = u[l] + courant * (
-                slope_h[l] - turn * v[l] + (u[l] * slope_u[l] + v[l] * (ua - ub)))
-            powers[0, s, 2, l, tall, :] = v[l] + courant * (
-                (ha - hb) + turn * u[l] + (u[l] * slope_v[l] + v[l] * (va - vb)))
-        return carry
-
-    lax.fori_loop(0, 2, start_fields, 0)
-
-    slot = jnp.where(last, 2, 1)
-    factor = jnp.where(last, -WRAPS, -1.0).astype(F32)
-    for f in range(3):
-        for l in range(3):
-            powers[0, 2, f, l, tall, :] = factor * state[slot, f, l, tall, :]
-            powers[0, 1, f, l, tall, :] = powers[0, 1, f, l, tall, :] - state[0, f, l, tall, :]
-
-    def next_power(m, carry):
-        for q in range(3):
-            h = [powers[m, q, 0, l, tall, :] for l in range(3)]
-            u = [powers[m, q, 1, l, tall, :] for l in range(3)]
-            slope_h, slope_u = dx(h), dx(u)
-            turn = rotation[...]
+    def all_powers(start, count, block_start, block_count):
+        def at(first_row, rows):
+            begin = pl.multiple_of(EDGE + first_row, 8)
+            return pl.ds(begin, rows), pl.ds(begin + 1, rows), pl.ds(begin - 1, rows)
+
+        tall, above, below = at(start, count)
+        turns = pl.ds(pl.multiple_of(start, 8), count)
+
+        def start_fields(s, carry):
+            h = [state[s, 0, l, tall, :] for l in range(3)]
+            u = [state[s, 1, l, tall, :] for l in range(3)]
+            v = [state[s, 2, l, tall, :] for l in range(3)]
+            turn = rotation[turns, :]
+            flux = dx([u[l] + h[l] * u[l] for l in range(3)])
+            slope_h, slope_u, slope_v = dx(h), dx(u), dx(v)
             for l in range(3):
-                ha, hb = powers[m, q, 0, l, above, :], powers[m, q, 0, l, below, :]
-                va, vb = powers[m, q, 2, l, above, :], powers[m, q, 2, l, below, :]
-                v = powers[m, q, 2, l, tall, :]
-                powers[m + 1, q, 0, l, tall, :] = slope_u[l] + (va - vb)
-                powers[m + 1, q, 1, l, tall, :] = slope_h[l] - turn * v
-                powers[m + 1, q, 2, l, tall, :] = (ha - hb) + turn * u[l]
-        return carry
-
-    lax.fori_loop(0, CHEB - 1, next_power, 0)
-
-    block, block_up, block_down = pl.ds(BASE, ROWS), pl.ds(BASE + 1, ROWS), pl.ds(BASE - 1, ROWS)
-    m = CHEB - 1
-    for q in range(3):
-        h = [powers[m, q, 0, l, block, :] for l in range(3)]
-        u = [powers[m, q, 1, l, block, :] for l in range(3)]
-        slope_h, slope_u = dx(h), dx(u)
-        turn = rotation[pl.ds(HALO, ROWS), :]
-        for l in range(2):
-            ha, hb = powers[m, q, 0, l, block_up, :], powers[m, q, 0, l, block_down, :]
-            va, vb = powers[m, q, 2, l, block_up, :], powers[m, q, 2, l, block_down, :]
-            v = powers[m, q, 2, l, block, :]
-            powers[m + 1, q, 0, l, block, :] = slope_u[l] + (va - vb)
-            powers[m + 1, q, 1, l, block, :] = slope_h[l] - turn * v
-            powers[m + 1, q, 2, l, block, :] = (ha - hb) + turn * u[l]
-
-    def mix(f, wanted):
+                (ha, hb), (ua, ub), (va, vb) = [(state[s, f, l, above, :], state[s, f, l, below, :]) for f in range(3)]
+                powers[0, s, 0, l, tall, :] = h[l] + courant * (flux[l] + ((va + ha * va) - (vb + hb * vb)))
+                powers[0, s, 1, l, tall, :] = u[l] + courant * (
+                    slope_h[l] - turn * v[l] + (u[l] * slope_u[l] + v[l] * (ua - ub)))
+                powers[0, s, 2, l, tall, :] = v[l] + courant * (
+                    (ha - hb) + turn * u[l] + (u[l] * slope_v[l] + v[l] * (va - vb)))
+            return carry
+
+        lax.fori_loop(0, 2, start_fields, 0)
+
+        slot = jnp.where(last, 2, 1)
+        factor = jnp.where(last, -WRAPS, -1.0).astype(F32)
+        for f in range(3):
+            for l in range(3):
+                powers[0, 2, f, l, tall, :] = factor * state[slot, f, l, tall, :]
+                powers[0, 1, f, l, tall, :] = powers[0, 1, f, l, tall, :] - state[0, f, l, tall, :]
+
+        def apply(m, rows, turns, tiles):
+            here, up, down = rows
+            for q in range(3):
+                h = [powers[m, q, 0, l, here, :] for l in range(3)]
+                u = [powers[m, q, 1, l, here, :] for l in range(3)]
+                slope_h, slope_u = dx(h), dx(u)
+                turn = rotation[turns, :]
+                for l in range(tiles):
+                    ha, hb = powers[m, q, 0, l, up, :], powers[m, q, 0, l, down, :]
+                    va, vb = powers[m, q, 2, l, up, :], powers[m, q, 2, l, down, :]
+                    v = powers[m, q, 2, l, here, :]
+                    powers[m + 1, q, 0, l, here, :] = slope_u[l] + (va - vb)
+                    powers[m + 1, q, 1, l, here, :] = slope_h[l] - turn * v
+                    powers[m + 1, q, 2, l, here, :] = (ha - hb) + turn * u[l]
+
+        def next_power(m, carry):
+            apply(m, (tall, above, below), turns, 3)
+            return carry
+
+        lax.fori_loop(0, CHEB - 1, next_power, 0)
+        apply(CHEB - 1, at(HALO + block_start, block_count), pl.ds(pl.multiple_of(HALO + block_start, 8), block_count), 2)
+
+    most, rest = REST * (1 - late), MOST * late
+    await_bytes(y_bytes, HALO_Y)
+    await_side(1 - late)
+    spread_edges(HALO * (1 - late), TALL - HALO)
+    all_powers(HALO * (1 - late), TALL - HALO, most, MOST)
+
+    block = pl.ds(BASE, ROWS)
+
+    class Part:
+        def __init__(self, start, count):
+            self.rows = pl.ds(pl.multiple_of(start, 8), count)
+            self.source = pl.ds(pl.multiple_of(BASE + start, 8), count)
+            self.size = pl.ds(0, count)
+
+    large, small, whole = Part(most, MOST), Part(rest, REST), Part(0, ROWS)
+
+    def mix(part, f, wanted):
         def body(l, carry):
             totals = [None] * len(wanted)
             for q in range(3):
                 for m in range(CHEB + 1):
-                    value = powers[m, q, f, l, block, :]
+                    value = powers[m, q, f, l, part.source, :]
                     for i, (delta, p, _, _) in enumerate(wanted):
                         term = weight(delta, p, q, m) * value
                         totals[i] = term if totals[i] is None else totals[i] + term
             for (delta, p, ref, index), total in zip(wanted, totals, strict=True):
                 if delta:
                     total = total * jnp.where(tm + delta >= n_tm, circulant, 1.0).astype(F32)
-                ref[(*index, l)] = total
+                ref[(*index, l, part.rows, slice(None))] = total
             return carry
         lax.fori_loop(0, 2, body, 0)
 
     def both_steps(delta, ref, *index):
         return [(delta, p, ref, (*index, p)) for p in range(2)]
 
-    def send_across(place, f):
-        i = {0: CROSS_OWN, 1: CROSS_NEAR + f, 2: CROSS_FAR + f, 3: CROSS_NEAR + f}[place]
-        remote(cross.at[place, f], crossed.at[place, f], sem.at[CROSS_S], sem.at[i], (partner, gx, gy)).start()
-
     def odd_delta(seat, place):
         return (2 * place + 1 - 2 * seat) % 8
 
-    def for_partner(f, places):
+    def for_partner(part, f, places):
         for seat in range(2):
             @pl.when(core == seat)
             def _(seat=seat):
-                mix(f, [w for place in places for w in both_steps(odd_delta(seat, place), cross, place, f)])
-        for place in places:
-            send_across(place, f)
+                mix(part, f, [w for place in places for w in both_steps(odd_delta(seat, place), cross, place, f)])
+
+    def send_across(part, f, place, i):
+        remote(cross.at[place, f, :, :, part.rows, :], crossed.at[place, f, :, :, part.rows, :], sem.at[CROSS_S], sem.at[i],
+               (partner, gx, gy)).start()
 
     up, down = (chip_up, gx, gy), (chip_down, gx, gy)
 
     def send_ring(i, side, src, dst):
         remote(src, dst, sem.at[RING_S], sem.at[i], down if side else up).start()
 
-    def far_odd(f, carry):
-        for_partner(f, (2,))
-        return carry
-
-    def far_even(f, carry):
-        mix(f, both_steps(4, own, 0, f))
-        return carry
-
-    def far_out(f, carry):
-        for_partner(f, (1, 3))
-        await_bytes(crossed.at[2, f], CROSS_FAR + f)
-        own[0, f] = own[0, f] + crossed[2, f]
+    def add_into(part, f, place, i, other):
+        own[i, f, :, :, part.rows, :] = own[i, f, :, :, part.rows, :] + crossed[other, f, :, :, part.rows, :]
+
+    def send_far(part, f, i):
         for side in range(2):
-            send_ring(RING_FAR + f, side, own.at[0, f, side], relay.at[side, f])
-        return carry
-
-    def near_out(f, carry):
-        mix(f, both_steps(2, own, 1, f) + both_steps(6, own, 2, f))
-        await_bytes(crossed.at[pl.ds(0, 2), f], CROSS_NEAR + f)
-        own[1, f] = own[1, f] + crossed[1, f]
-        own[2, f] = own[2, f] + crossed[3, f]
+            send_ring(i, side, own.at[0, f, side, :, part.rows, :], relay.at[side, f, :, part.rows, :])
+
+    def send_near(part, f, i):
         for side in range(2):
-            send_ring(RING_END + f, side, own.at[1 + side, f, 1 - side], near_a.at[side, f])
-        return carry
-
-    def here_odd(f, carry):
-        for_partner(f, (0,))
-        return carry
-
-    def here_even(f, carry):
-        mix(f, both_steps(0, own, 3, f))
-        return carry
-
-    def relay_out(f, carry):
-        await_bytes(relay.at[:, f], RING_FAR + f)
+            send_ring(i, side, own.at[1 + side, f, 1 - side, :, part.rows, :], near_a.at[side, f, :, part.rows, :])
+
+    def send_relayed(part, f, i):
         for side in range(2):
-            own[1 + side, f, side] = own[1 + side, f, side] + relay[side, f]
-            send_ring(RING_END + f, side, own.at[1 + side, f, side], near_b.at[side, f])
-        return carry
-
-    lax.fori_loop(0, 3, far_odd, 0)
-    lax.fori_loop(0, 3, far_even, 0)
-    lax.fori_loop(0, 3, far_out, 0)
-    lax.fori_loop(0, 3, near_out, 0)
-    lax.fori_loop(0, 3, here_odd, 0)
-    lax.fori_loop(0, 3, here_even, 0)
-    lax.fori_loop(0, 3, relay_out, 0)
+            send_ring(i, side, own.at[1 + side, f, side, :, part.rows, :], near_b.at[side, f, :, part.rows, :])
+
+    def add_relayed(part, f):
+        for side in range(2):
+            own[1 + side, f, side, :, part.rows, :] = (
+                own[1 + side, f, side, :, part.rows, :] + relay[side, f, :, part.rows, :])
+
+    def each_field(body):
+        def step(f, carry):
+            body(f)
+            return carry
+        lax.fori_loop(0, 3, step, 0)
+
+    def far_odd(f):
+        for_partner(large, f, (2,))
+        send_across(large, f, 2, CROSS_FAR + f)
+
+    def far_out(f):
+        for_partner(large, f, (1, 3))
+        send_across(large, f, 1, CROSS_NEAR + f)
+        send_across(large, f, 3, CROSS_NEAR + f)
+        await_bytes(crossed.at[2, f, :, :, large.size, :], CROSS_FAR + f)
+        add_into(large, f, 2, 0, 2)
+        send_far(large, f, RING_FAR + f)
+
+    def near_out(f):
+        mix(large, f, both_steps(2, own, 1, f) + both_steps(6, own, 2, f))
+        await_bytes(crossed.at[pl.ds(0, 2), f, :, :, large.size, :], CROSS_NEAR + f)
+        add_into(large, f, 1, 1, 1)
+        add_into(large, f, 3, 2, 3)
+        send_near(large, f, RING_END + f)
+
+    def relay_out(f):
+        await_bytes(relay.at[:, f, :, large.size, :], RING_FAR + f)
+        add_relayed(large, f)
+        send_relayed(large, f, RING_END + f)
+
+    def here_odd(f):
+        for_partner(whole, f, (0,))
+        send_across(whole, f, 0, CROSS_OWN)
+
+    each_field(far_odd)
+    each_field(lambda f: mix(large, f, both_steps(4, own, 0, f)))
+    each_field(far_out)
+
+    await_side(late)
+    spread_edges((HALO + ROWS) * late, HALO)
+    all_powers(ROWS * late, 2 * HALO, rest, REST)
+
+    fields = slice(None)
+    each_field(lambda f: for_partner(small, f, (2,)))
+    send_across(small, fields, 2, CROSS_FAR + 3)
+    each_field(near_out)
+    each_field(lambda f: mix(small, f, both_steps(4, own, 0, f)))
+    await_bytes(crossed.at[2, :, :, :, small.size, :], CROSS_FAR + 3)
+    add_into(small, fields, 2, 0, 2)
+    send_far(small, fields, RING_FAR + 3)
+    each_field(lambda f: for_partner(small, f, (1, 3)))
+    send_across(small, fields, 1, CROSS_NEAR + 3)
+    send_across(small, fields, 3, CROSS_NEAR + 3)
+    each_field(lambda f: mix(small, f, both_steps(2, own, 1, f) + both_steps(6, own, 2, f)))
+    each_field(relay_out)
+    await_bytes(crossed.at[pl.ds(0, 2), :, :, :, small.size, :], CROSS_NEAR + 3)
+    add_into(small, fields, 1, 1, 1)
+    add_into(small, fields, 3, 2, 3)
+    send_near(small, fields, RING_END + 3)
+    each_field(here_odd)
+    await_bytes(relay.at[:, :, :, small.size, :], RING_FAR + 3)
+    add_relayed(small, fields)
+    send_relayed(small, fields, RING_END + 3)
+    each_field(lambda f: mix(whole, f, both_steps(0, own, 3, f)))
 
     await_bytes(prev, PASS_R)
     await_bytes(crossed.at[0], CROSS_OWN)
@@ -380,14 +438,19 @@
     await_bytes(prev, PASS_S)
     await_bytes(cross, CROSS_S)
 
-    def finish(f, carry):
-        await_bytes(own.at[pl.ds(0, 2), f], RING_END + f)
-        for l in range(2):
-            out_buf[0, f, l] = out_buf[0, f, l] - (near_b[0, f, l] + near_a[1, f, l])
-            out_buf[1, f, l] = out_buf[1, f, l] - (near_a[0, f, l] + near_b[1, f, l])
-        return carry
-
-    lax.fori_loop(0, 3, finish, 0)
+    def finish(part, f):
+        rows = part.rows
+        for p in range(2):
+            out_buf[p, f, :, rows, :] = out_buf[p, f, :, rows, :] - (
+                near_b[p, f, :, rows, :] + near_a[1 - p, f, :, rows, :])
+
+    def finish_large(f):
+        await_bytes(own.at[pl.ds(0, 2), f, :, :, large.size, :], RING_END + f)
+        finish(large, f)
+
+    each_field(finish_large)
+    await_bytes(own.at[pl.ds(0, 2), :, :, :, small.size, :], RING_END + 3)
+    finish(small, fields)
     await_bytes(own.at[pl.ds(0, 3)], RING_S)
 
 
@@ -424,6 +487,7 @@
             pltpu.VMEM((ROWS, 128), F32),
             pltpu.VMEM((TALL, 128), F32),
             pltpu.VMEM((TALL, 128), F32),
+            pltpu.VMEM((2, 3, 3, 2, HALO, 128), F32),
             pltpu.VMEM((4, 3, 2, 2, ROWS, 128), F32),
             pltpu.VMEM((4, 3, 2, 2, ROWS, 128), F32),
             pltpu.VMEM((4, 3, 2, 2, ROWS, 128), F32),

time: 28.4 us -> 26.5 us (0.933)
  Pallas kernels: 27.6 us -> 25.8 us
    pallas_call x1, Pallas kernels: 26.8 us -> 25 us  [shards(): pl.pallas_call(kernel, out_shape=(tiles, tiles), in_specs=[slow, slow], o...]
where the time goes in v4:
time: 26.5 us; the launch traced here: 26.4 us
  Pallas kernels  25.8 us (97%)
  between operations  0.64 us (2%)
    pallas_call x1, Pallas kernels, shards(): pl.pallas_call(kernel, out_shape=(tiles, tiles), in_specs=[slow, slow], o...  25 us
    pallas_call x1, Pallas kernels, shards(): pl.pallas_call(put_out, out_shape=(whole, whole), in_specs=[anywhere, any...  0.78 us

profile of v4, /device:TPU:1, one launch (start us, length us, event | category | flops | bytes accessed | tf_op | source)
XLA Modules:
  0.0 26.4 jit_solution(17824352939051845394)
XLA Ops:
  0.6 25.0 %paradiag.1 = (f32[2,3,2,32,128]{4,3,2,1,0:T(8,128)S(1)}, f32[2,3,2,32,128]{4,3,2,1,0:T(8,128)S(1)}) custom-call(f32[2,3,32,256]{3,2,1,0:T(8,128)} %traj.1, f32[3,32,256]{2,1,0:T(8,128)} %init.1), custom_call_target="tpu_custom_call" | custom-call | tf_op jit(solution)/shard_map/paradiag/pallas_call | solution.py:476
  25.6 0.8 %put_out.1 = (f32[2,3,32,256]{3,2,1,0:T(8,128)}, f32[2,3,32,256]{3,2,1,0:T(8,128)}) custom-call(f32[2,3,2,32,128]{4,3,2,1,0:T(8,128)S(1)} %get-tuple-element.4.upd_in, f32[2,3,2,32,128]{4,3,2,1,0:T(8,128)S(1)} %get-tuple-element.5.res_in), custom_call_target="tpu_custom_call" | custom-call | tf_op jit(solution)/shard_map/put_out/pallas_call | solution.py:503

commit v5 on v4

--- a/solution.py
+++ b/solution.py
@@ -250,7 +250,8 @@
                     (ha - hb) + turn * u[l] + (u[l] * slope_v[l] + v[l] * (va - vb)))
             return carry
 
-        lax.fori_loop(0, 2, start_fields, 0)
+        for s in range(2):
+            start_fields(s, 0)
 
         slot = jnp.where(last, 2, 1)
         factor = jnp.where(last, -WRAPS, -1.0).astype(F32)
@@ -278,7 +279,8 @@
             apply(m, (tall, above, below), turns, 3)
             return carry
 
-        lax.fori_loop(0, CHEB - 1, next_power, 0)
+        for m in range(CHEB - 1):
+            next_power(m, 0)
         apply(CHEB - 1, at(HALO + block_start, block_count), pl.ds(pl.multiple_of(HALO + block_start, 8), block_count), 2)
 
     most, rest = REST * (1 - late), MOST * late
@@ -311,7 +313,8 @@
                     total = total * jnp.where(tm + delta >= n_tm, circulant, 1.0).astype(F32)
                 ref[(*index, l, part.rows, slice(None))] = total
             return carry
-        lax.fori_loop(0, 2, body, 0)
+        for l in range(2):
+            body(l, 0)
 
     def both_steps(delta, ref, *index):
         return [(delta, p, ref, (*index, p)) for p in range(2)]

time: 26.5 us -> 25.3 us (0.955)
  Pallas kernels: 25.8 us -> 24.5 us
    pallas_call x1, Pallas kernels: 25 us -> 23.7 us  [shards(): pl.pallas_call(kernel, out_shape=(tiles, tiles), in_specs=[slow, slow], o...]
where the time goes in v5:
time: 25.3 us; the launch traced here: 25.1 us
  Pallas kernels  24.5 us (97%)
  between operations  0.64 us (3%)
    pallas_call x1, Pallas kernels, shards(): pl.pallas_call(kernel, out_shape=(tiles, tiles), in_specs=[slow, slow], o...  23.7 us
    pallas_call x1, Pallas kernels, shards(): pl.pallas_call(put_out, out_shape=(whole, whole), in_specs=[anywhere, any...  0.78 us

profile of v5, /device:TPU:1, one launch (start us, length us, event | category | flops | bytes accessed | tf_op | source)
XLA Modules:
  0.0 25.1 jit_solution(15495082686978102507)
XLA Ops:
  0.6 23.7 %paradiag.1 = (f32[2,3,2,32,128]{4,3,2,1,0:T(8,128)S(1)}, f32[2,3,2,32,128]{4,3,2,1,0:T(8,128)S(1)}) custom-call(f32[2,3,32,256]{3,2,1,0:T(8,128)} %traj.1, f32[3,32,256]{2,1,0:T(8,128)} %init.1), custom_call_target="tpu_custom_call" | custom-call | tf_op jit(solution)/shard_map/paradiag/pallas_call | solution.py:479
  24.4 0.8 %put_out.1 = (f32[2,3,32,256]{3,2,1,0:T(8,128)}, f32[2,3,32,256]{3,2,1,0:T(8,128)}) custom-call(f32[2,3,2,32,128]{4,3,2,1,0:T(8,128)S(1)} %get-tuple-element.4.upd_in, f32[2,3,2,32,128]{4,3,2,1,0:T(8,128)S(1)} %get-tuple-element.5.res_in), custom_call_target="tpu_custom_call" | custom-call | tf_op jit(solution)/shard_map/put_out/pallas_call | solution.py:506

commit v6 on v5

--- a/solution.py
+++ b/solution.py
@@ -29,7 +29,7 @@
 OPPOSITE = (1, 0, 5, 6, 7, 2, 3, 4, 8, 8, 8, 8)
 MOST, REST = 24, 8
 (LOAD, HALO_S, HALO_Y, HALO_SIDE, OPEN_S, OPEN_SIDE, PASS_S, PASS_R, CROSS_S, RING_S, CROSS_FAR, CROSS_NEAR, CROSS_OWN, RING_FAR,
- RING_END, N_SEM) = (0, 1, 2, 3, 5, 6, 8, 9, 10, 11, 12, 16, 20, 21, 25, 29)
+ RING_END, N_SEM) = (0, 1, 2, 3, 5, 6, 8, 9, 10, 11, 12, 16, 20, 21, 25, 26)
 
 
 def power_table():
@@ -92,16 +92,28 @@
         load.start()
     loaded = state.at[:, :, pl.ds(0, 2), pl.ds(BASE, ROWS), :]
 
-    def arrival(t, x, y):
-        by_z = jnp.minimum(2 * y + 2 * jnp.minimum(y, 1), 11)
-        return (t // 2 + x + by_z + 1 - t % 2) * 256 + t * 32 + x * 8 + y
-
     across = jnp.where(core == 1, after, before)
     peers = [(tm, east, gy), (tm, west, gy), (tm, gx, north), (tm, east, north), (tm, west, north),
              (tm, gx, south), (tm, west, south), (tm, east, south),
              (partner, gx, gy), (chip_up, gx, gy), (chip_down, gx, gy), (across, gx, gy)]
-    mine = arrival(tm, gx, gy)
-    earlier = [(arrival(*peer) < mine).astype(jnp.int32) for peer in peers]
+    chip = lax.div(tm, 2)
+    next_chip, prior_chip = lax.rem(chip + 1, n_tm // 2), lax.rem(chip + n_tm // 2 - 1, n_tm // 2)
+
+    def key_t(its_chip, its_core):
+        return (its_chip + 1 - its_core) * 256 + (2 * its_chip + its_core) * 32
+
+    def key_z(y):
+        return jnp.minimum(2 * y + 2 * jnp.minimum(y, 1), 11) * 256 + y
+
+    mine_t, mine_x, mine_z = key_t(chip, core), gx * 264, key_z(gy)
+    east_x, west_x, north_z, south_z = east * 264, west * 264, key_z(north), key_z(south)
+    mine = mine_t + mine_x + mine_z
+    keys = [mine_t + east_x + mine_z, mine_t + west_x + mine_z, mine_t + mine_x + north_z, mine_t + east_x + north_z,
+            mine_t + west_x + north_z, mine_t + mine_x + south_z, mine_t + west_x + south_z, mine_t + east_x + south_z,
+            key_t(chip, 1 - core) + mine_x + mine_z, key_t(next_chip, core) + mine_x + mine_z,
+            key_t(prior_chip, core) + mine_x + mine_z,
+            key_t(jnp.where(core == 1, next_chip, prior_chip), 1 - core) + mine_x + mine_z]
+    earlier = [(key < mine).astype(jnp.int32) for key in keys]
 
     barrier = pltpu.get_barrier_semaphore()
     for peer, sooner in zip(peers, earlier, strict=True):
@@ -167,16 +179,23 @@
         @pl.when(earlier[i] == 1)
         def _(i=i):
             halo[i].start()
+    def send_to_later(i):
+        pl.semaphore_wait(ready.at[i], 1)
+        halo[i].start()
+
+    at_end = 1 - jnp.minimum(gy, 1)
     for i in range(8):
-        @pl.when(earlier[i] == 0)
+        @pl.when(earlier[i] + (at_end if i >= 5 else 0) == 0)
         def _(i=i):
-            pl.semaphore_wait(ready.at[i], 1)
-            halo[i].start()
+            send_to_later(i)
 
     @pl.when(last)
     def _():
-        for copy in opening:
-            copy.start()
+        opening[0].start()
+
+        @pl.when(gy > 0)
+        def _():
+            opening[1].start()
 
     later_count = 4 - sum(earlier[8:])
 
@@ -193,7 +212,7 @@
     side_bytes = powers.at[:, 0, 0, 0, pl.ds(0, 2 * HALO), :]
     opening_bytes, opening_side = state.at[2, :, cols, pl.ds(0, 2 * HALO), :], state.at[2, :, cols, pl.ds(0, HALO), :]
 
-    late = jnp.minimum(gy, 1) * jnp.minimum(n_gy - 1 - gy, 1)
+    late = jnp.minimum(gy, 1)
 
     def await_side(side):
         await_bytes(side_bytes, HALO_SIDE + side)
@@ -288,6 +307,17 @@
     await_side(1 - late)
     spread_edges(HALO * (1 - late), TALL - HALO)
     all_powers(HALO * (1 - late), TALL - HALO, most, MOST)
+
+    for i in range(5, 8):
+        @pl.when((1 - earlier[i]) * at_end == 1)
+        def _(i=i):
+            send_to_later(i)
+
+    @pl.when(last)
+    def _():
+        @pl.when(gy == 0)
+        def _():
+            opening[1].start()
 
     block = pl.ds(BASE, ROWS)
 
@@ -380,12 +410,12 @@
         await_bytes(crossed.at[pl.ds(0, 2), f, :, :, large.size, :], CROSS_NEAR + f)
         add_into(large, f, 1, 1, 1)
         add_into(large, f, 3, 2, 3)
-        send_near(large, f, RING_END + f)
+        send_near(large, f, RING_END)
 
     def relay_out(f):
         await_bytes(relay.at[:, f, :, large.size, :], RING_FAR + f)
         add_relayed(large, f)
-        send_relayed(large, f, RING_END + f)
+        send_relayed(large, f, RING_END)
 
     def here_odd(f):
         for_partner(whole, f, (0,))
@@ -415,11 +445,11 @@
     await_bytes(crossed.at[pl.ds(0, 2), :, :, :, small.size, :], CROSS_NEAR + 3)
     add_into(small, fields, 1, 1, 1)
     add_into(small, fields, 3, 2, 3)
-    send_near(small, fields, RING_END + 3)
+    send_near(small, fields, RING_END)
     each_field(here_odd)
     await_bytes(relay.at[:, :, :, small.size, :], RING_FAR + 3)
     add_relayed(small, fields)
-    send_relayed(small, fields, RING_END + 3)
+    send_relayed(small, fields, RING_END)
     each_field(lambda f: mix(whole, f, both_steps(0, own, 3, f)))
 
     await_bytes(prev, PASS_R)
@@ -441,19 +471,9 @@
     await_bytes(prev, PASS_S)
     await_bytes(cross, CROSS_S)
 
-    def finish(part, f):
-        rows = part.rows
-        for p in range(2):
-            out_buf[p, f, :, rows, :] = out_buf[p, f, :, rows, :] - (
-                near_b[p, f, :, rows, :] + near_a[1 - p, f, :, rows, :])
-
-    def finish_large(f):
-        await_bytes(own.at[pl.ds(0, 2), f, :, :, large.size, :], RING_END + f)
-        finish(large, f)
-
-    each_field(finish_large)
-    await_bytes(own.at[pl.ds(0, 2), :, :, :, small.size, :], RING_END + 3)
-    finish(small, fields)
+    await_bytes(own.at[pl.ds(0, 2)], RING_END)
+    for p in range(2):
+        out_buf[p] = out_buf[p] - (near_b[p] + near_a[1 - p])
     await_bytes(own.at[pl.ds(0, 3)], RING_S)
 
 

time: 25.3 us -> 24.3 us (0.960)
  Pallas kernels: 24.5 us -> 23.6 us
    pallas_call x1, Pallas kernels: 23.7 us -> 22.8 us  [shards(): pl.pallas_call(kernel, out_shape=(tiles, tiles), in_specs=[slow, slow], o...]
where the time goes in v6:
time: 24.3 us; the launch traced here: 24.2 us
  Pallas kernels  23.6 us (97%)
  between operations  0.64 us (3%)
    pallas_call x1, Pallas kernels, shards(): pl.pallas_call(kernel, out_shape=(tiles, tiles), in_specs=[slow, slow], o...  22.8 us
    pallas_call x1, Pallas kernels, shards(): pl.pallas_call(put_out, out_shape=(whole, whole), in_specs=[anywhere, any...  0.78 us

profile of v6, /device:TPU:1, one launch (start us, length us, event | category | flops | bytes accessed | tf_op | source)
XLA Modules:
  0.0 24.2 jit_solution(3066434963874773704)
XLA Ops:
  0.6 22.8 %paradiag.1 = (f32[2,3,2,32,128]{4,3,2,1,0:T(8,128)S(1)}, f32[2,3,2,32,128]{4,3,2,1,0:T(8,128)S(1)}) custom-call(f32[2,3,32,256]{3,2,1,0:T(8,128)} %traj.1, f32[3,32,256]{2,1,0:T(8,128)} %init.1), custom_call_target="tpu_custom_call" | custom-call | tf_op jit(solution)/shard_map/paradiag/pallas_call | solution.py:499
  23.5 0.8 %put_out.1 = (f32[2,3,32,256]{3,2,1,0:T(8,128)}, f32[2,3,32,256]{3,2,1,0:T(8,128)}) custom-call(f32[2,3,2,32,128]{4,3,2,1,0:T(8,128)S(1)} %get-tuple-element.4.upd_in, f32[2,3,2,32,128]{4,3,2,1,0:T(8,128)S(1)} %get-tuple-element.5.res_in), custom_call_target="tpu_custom_call" | custom-call | tf_op jit(solution)/shard_map/put_out/pallas_call | solution.py:526

commit v7 on v6

--- a/solution.py
+++ b/solution.py
@@ -26,7 +26,7 @@
 BASE = EDGE + HALO
 DEEP = TALL + 2 * EDGE
 WRAPS = 1.0 / circulant
-OPPOSITE = (1, 0, 5, 6, 7, 2, 3, 4, 8, 8, 8, 8)
+OPPOSITE = (1, 0, 5, 6, 7, 2, 3, 4, 8, 8, 8, 8, 8)
 MOST, REST = 24, 8
 (LOAD, HALO_S, HALO_Y, HALO_SIDE, OPEN_S, OPEN_SIDE, PASS_S, PASS_R, CROSS_S, RING_S, CROSS_FAR, CROSS_NEAR, CROSS_OWN, RING_FAR,
  RING_END, N_SEM) = (0, 1, 2, 3, 5, 6, 8, 9, 10, 11, 12, 16, 20, 21, 25, 26)
@@ -68,7 +68,7 @@
 def kernel(
     traj, init, out_buf, res_buf,
     state, powers, rotation, prev, strip_l, strip_r, edge_l, edge_r,
-    side_in, cross, crossed, own, relay, near_a, near_b,
+    side_in, cross, crossed, own, relay, relay_odd, near_a, near_b,
     ready, sem,
 ):
     tm, gx, gy = lax.axis_index("tm"), lax.axis_index("gx"), lax.axis_index("gy")
@@ -76,7 +76,7 @@
     core = lax.rem(tm, 2)
     east, west = lax.rem(gx + 1, n_gx), lax.rem(gx + n_gx - 1, n_gx)
     north, south = lax.rem(gy + 1, n_gy), lax.rem(gy + n_gy - 1, n_gy)
-    after, before = lax.rem(tm + 1, n_tm), lax.rem(tm + n_tm - 1, n_tm)
+    after = lax.rem(tm + 1, n_tm)
     chip_up, chip_down = lax.rem(tm + 2, n_tm), lax.rem(tm + n_tm - 2, n_tm)
     partner = tm + 1 - 2 * core
     last = tm == n_tm - 1
@@ -92,10 +92,10 @@
         load.start()
     loaded = state.at[:, :, pl.ds(0, 2), pl.ds(BASE, ROWS), :]
 
-    across = jnp.where(core == 1, after, before)
+    up_other, down_other = chip_up + 1 - 2 * core, chip_down + 1 - 2 * core
     peers = [(tm, east, gy), (tm, west, gy), (tm, gx, north), (tm, east, north), (tm, west, north),
              (tm, gx, south), (tm, west, south), (tm, east, south),
-             (partner, gx, gy), (chip_up, gx, gy), (chip_down, gx, gy), (across, gx, gy)]
+             (partner, gx, gy), (chip_up, gx, gy), (chip_down, gx, gy), (up_other, gx, gy), (down_other, gx, gy)]
     chip = lax.div(tm, 2)
     next_chip, prior_chip = lax.rem(chip + 1, n_tm // 2), lax.rem(chip + n_tm // 2 - 1, n_tm // 2)
 
@@ -112,7 +112,7 @@
             mine_t + west_x + north_z, mine_t + mine_x + south_z, mine_t + west_x + south_z, mine_t + east_x + south_z,
             key_t(chip, 1 - core) + mine_x + mine_z, key_t(next_chip, core) + mine_x + mine_z,
             key_t(prior_chip, core) + mine_x + mine_z,
-            key_t(jnp.where(core == 1, next_chip, prior_chip), 1 - core) + mine_x + mine_z]
+            key_t(next_chip, 1 - core) + mine_x + mine_z, key_t(prior_chip, 1 - core) + mine_x + mine_z]
     earlier = [(key < mine).astype(jnp.int32) for key in keys]
 
     barrier = pltpu.get_barrier_semaphore()
@@ -135,19 +135,6 @@
     pltpu.make_async_copy(loaded, loaded, sem.at[LOAD]).wait()
 
     lane_id = lax.broadcasted_iota(jnp.int32, (TALL, 128), 1)
-    packed_l = jnp.zeros((ROWS, 128), F32)
-    packed_r = jnp.zeros((ROWS, 128), F32)
-    for s in range(3):
-        for f in range(3):
-            spot = 8 * (3 * s + f)
-            here = (lane_id[:ROWS] >= spot) & (lane_id[:ROWS] < spot + 8)
-            left = state[s, f, 0, pl.ds(BASE, ROWS), :]
-            right = state[s, f, 1, pl.ds(BASE, ROWS), :]
-            packed_l = jnp.where(here, pltpu.roll(left, spot, 1) if spot else left, packed_l)
-            packed_r = jnp.where(here, pltpu.roll(right, spot + 8, 1), packed_r)
-    strip_l[...] = packed_l
-    strip_r[...] = packed_r
-
     def remote(src, dst, send, recv, peer):
         return pltpu.make_async_remote_copy(
             src_ref=src, dst_ref=dst, send_sem=send, recv_sem=recv, device_id=peer, device_id_type=MESH)
@@ -175,10 +162,30 @@
                (tm, gx, south)),
     ]
     passed = remote(state.at[1, :, cols, pl.ds(BASE, ROWS), :], prev, sem.at[PASS_S], sem.at[PASS_R], (after, gx, gy))
-    for i in range(8):
+    def send_to_earlier(i):
         @pl.when(earlier[i] == 1)
-        def _(i=i):
+        def _():
             halo[i].start()
+
+    for i in (2, 5):
+        send_to_earlier(i)
+
+    packed_l = jnp.zeros((ROWS, 128), F32)
+    packed_r = jnp.zeros((ROWS, 128), F32)
+    for s in range(3):
+        for f in range(3):
+            spot = 8 * (3 * s + f)
+            here = (lane_id[:ROWS] >= spot) & (lane_id[:ROWS] < spot + 8)
+            left = state[s, f, 0, pl.ds(BASE, ROWS), :]
+            right = state[s, f, 1, pl.ds(BASE, ROWS), :]
+            packed_l = jnp.where(here, pltpu.roll(left, spot, 1) if spot else left, packed_l)
+            packed_r = jnp.where(here, pltpu.roll(right, spot + 8, 1), packed_r)
+    strip_l[...] = packed_l
+    strip_r[...] = packed_r
+
+    for i in (0, 1, 3, 4, 6, 7):
+        send_to_earlier(i)
+
     def send_to_later(i):
         pl.semaphore_wait(ready.at[i], 1)
         halo[i].start()
@@ -197,7 +204,7 @@
         def _():
             opening[1].start()
 
-    later_count = 4 - sum(earlier[8:])
+    later_count = 5 - sum(earlier[8:])
 
     @pl.when(later_count > 0)
     def _():
@@ -387,20 +394,23 @@
             own[1 + side, f, side, :, part.rows, :] = (
                 own[1 + side, f, side, :, part.rows, :] + relay[side, f, :, part.rows, :])
 
-    def each_field(body):
+    def each_field(body, start=0):
         def step(f, carry):
             body(f)
             return carry
-        lax.fori_loop(0, 3, step, 0)
+        lax.fori_loop(start, 3, step, 0)
 
     def far_odd(f):
         for_partner(large, f, (2,))
         send_across(large, f, 2, CROSS_FAR + f)
 
-    def far_out(f):
+    def near_odd(f):
         for_partner(large, f, (1, 3))
         send_across(large, f, 1, CROSS_NEAR + f)
         send_across(large, f, 3, CROSS_NEAR + f)
+
+    def far_out(f):
+        near_odd(f)
         await_bytes(crossed.at[2, f, :, :, large.size, :], CROSS_FAR + f)
         add_into(large, f, 2, 0, 2)
         send_far(large, f, RING_FAR + f)
@@ -412,6 +422,13 @@
         add_into(large, f, 3, 2, 3)
         send_near(large, f, RING_END)
 
+    def relay_first():
+        await_bytes(own.at[pl.ds(0, 2), 0, :, :, large.size, :], RING_FAR)
+        for side in range(2):
+            relay[side, 0, :, large.rows, :] = relay[side, 0, :, large.rows, :] + relay_odd[side, :, large.rows, :]
+        add_relayed(large, 0)
+        send_relayed(large, 0, RING_END)
+
     def relay_out(f):
         await_bytes(relay.at[:, f, :, large.size, :], RING_FAR + f)
         add_relayed(large, f)
@@ -421,9 +438,16 @@
         for_partner(whole, f, (0,))
         send_across(whole, f, 0, CROSS_OWN)
 
-    each_field(far_odd)
-    each_field(lambda f: mix(large, f, both_steps(4, own, 0, f)))
-    each_field(far_out)
+    for_partner(large, 0, (2,))
+    for side, other in enumerate((up_other, down_other)):
+        remote(cross.at[2, 0, side, :, large.rows, :], relay_odd.at[side, :, large.rows, :], sem.at[CROSS_S],
+               sem.at[RING_FAR], (other, gx, gy)).start()
+    mix(large, 0, both_steps(4, own, 0, 0))
+    send_far(large, 0, RING_FAR)
+    each_field(far_odd, 1)
+    each_field(lambda f: mix(large, f, both_steps(4, own, 0, f)), 1)
+    near_odd(0)
+    each_field(far_out, 1)
 
     await_side(late)
     spread_edges((HALO + ROWS) * late, HALO)
@@ -441,7 +465,8 @@
     send_across(small, fields, 1, CROSS_NEAR + 3)
     send_across(small, fields, 3, CROSS_NEAR + 3)
     each_field(lambda f: mix(small, f, both_steps(2, own, 1, f) + both_steps(6, own, 2, f)))
-    each_field(relay_out)
+    relay_first()
+    each_field(relay_out, 1)
     await_bytes(crossed.at[pl.ds(0, 2), :, :, :, small.size, :], CROSS_NEAR + 3)
     add_into(small, fields, 1, 1, 1)
     add_into(small, fields, 3, 2, 3)
@@ -515,6 +540,7 @@
             pltpu.VMEM((4, 3, 2, 2, ROWS, 128), F32),
             pltpu.VMEM((4, 3, 2, 2, ROWS, 128), F32),
             pltpu.VMEM((2, 3, 2, ROWS, 128), F32),
+            pltpu.VMEM((2, 2, ROWS, 128), F32),
             pltpu.VMEM((2, 3, 2, ROWS, 128), F32),
             pltpu.VMEM((2, 3, 2, ROWS, 128), F32),
             pltpu.SemaphoreType.REGULAR((9,)),

time: 24.3 us -> 23.9 us (0.984)
  Pallas kernels: 23.6 us -> 23.1 us
    pallas_call x1, Pallas kernels: 22.8 us -> 22.3 us  [shards(): pl.pallas_call(kernel, out_shape=(tiles, tiles), in_specs=[slow, slow], o...]
where the time goes in v7:
time: 23.9 us; the launch traced here: 23.7 us
  Pallas kernels  23.1 us (97%)
  between operations  0.64 us (3%)
    pallas_call x1, Pallas kernels, shards(): pl.pallas_call(kernel, out_shape=(tiles, tiles), in_specs=[slow, slow], o...  22.3 us
    pallas_call x1, Pallas kernels, shards(): pl.pallas_call(put_out, out_shape=(whole, whole), in_specs=[anywhere, any...  0.78 us

profile of v7, /device:TPU:1, one launch (start us, length us, event | category | flops | bytes accessed | tf_op | source)
XLA Modules:
  0.0 23.7 jit_solution(10394840140479896108)
XLA Ops:
  0.6 22.3 %paradiag.1 = (f32[2,3,2,32,128]{4,3,2,1,0:T(8,128)S(1)}, f32[2,3,2,32,128]{4,3,2,1,0:T(8,128)S(1)}) custom-call(f32[2,3,32,256]{3,2,1,0:T(8,128)} %traj.1, f32[3,32,256]{2,1,0:T(8,128)} %init.1), custom_call_target="tpu_custom_call" | custom-call | tf_op jit(solution)/shard_map/paradiag/pallas_call | solution.py:524
  23.0 0.8 %put_out.1 = (f32[2,3,32,256]{3,2,1,0:T(8,128)}, f32[2,3,32,256]{3,2,1,0:T(8,128)}) custom-call(f32[2,3,2,32,128]{4,3,2,1,0:T(8,128)S(1)} %get-tuple-element.4.upd_in, f32[2,3,2,32,128]{4,3,2,1,0:T(8,128)S(1)} %get-tuple-element.5.res_in), custom_call_target="tpu_custom_call" | custom-call | tf_op jit(solution)/shard_map/put_out/pallas_call | solution.py:552
